TPU v7x, 32 devices: a whole 2x2x4 slice. The times are simulated.
32 devices in a mesh: rows: 8 (over z, y), hosts: 4 (over x, core).
Axes of the slice: x: 2, y: 2, z: 4, core: 2. Of those that a mesh axis runs over, the one named last changes fastest.
Arguments:
- embeddings: float32 [32768, 768], P(('rows', 'hosts')), may hold values from -6 to 6
- root_centroids: float32 [512, 768], replicated, may hold values from -6 to 6
- member_ids: int32 [3, 32768], P(None, ('rows', 'hosts')), may hold values from 0 to 511
- split_order: int32 [3, 512], replicated, may hold values from 0 to 511, each once within a row
- seed_rows: int32 [3, 256, 2], replicated, may hold values from 0 to 32767
Outputs:
- centroids: float32 [512, 768], replicated
- spread: float32 [3, 512], replicated
- child_weight: float32 [3, 32768], P(None, ('rows', 'hosts'))
Inputs may be any that keep to these rules, and one draw needn't show every extreme that they name: Each row of split_order names every cluster number once; its first 256 entries are the clusters split at that level.
All inputs are finite; a program needn't handle non-finite values.
Results may differ from a plain program's by a relative error of at most 0.0003.
Values sent between devices are 32-bit elements; how exact they have to be, the bound alone decides.
No kernel may reach another device: no remote copies, remote signals or barrier semaphores. Data moves between devices by JAX's collectives and lax.ppermute only.
A program may use at most 64 MiB of HBM per device.

v0:
```python
import jax
import jax.numpy as jnp
from jax import lax
from jax.sharding import PartitionSpec as P


def finish(sums, counts, energy, seeds_flat, width):
    centre = (sums + seeds_flat) / (counts + 1.0)[:, None]
    error = (
        energy - 2.0 * jnp.sum(centre * sums, axis=1) + counts * jnp.sum(centre * centre, axis=1)
    )
    return (centre, error / ((counts + 1.0) * width))


def on_device(embeddings, root_centroids, member_ids, split_order, seed_rows):
    high = lax.Precision.HIGHEST
    rows_dev, width = embeddings.shape
    splits_count = seed_rows.shape[1]
    clusters = 2 * splits_count
    position = lax.axis_index("rows") * lax.axis_size("hosts") + lax.axis_index("hosts")
    first_row = position * rows_dev
    scale = 0.5 / jnp.sqrt(jnp.float32(width))
    squares = jnp.sum(embeddings * embeddings, axis=1)
    current = root_centroids
    spreads = []
    weights_out = []
    for level in range(seed_rows.shape[0]):
        splits = split_order[level, :splits_count]
        parent = jnp.take(current, splits, axis=0)
        local = seed_rows[level] - first_row
        inside = (local >= 0) & (local < rows_dev)
        picked = jnp.take(embeddings, jnp.clip(local, 0, rows_dev - 1), axis=0)
        fetched = lax.psum(
            jnp.where(inside[..., None], picked, jnp.float32(0.0)), ("rows", "hosts")
        )
        seeds = 0.5 * (parent[:, None, :] + fetched)
        delta = seeds[:, 0, :] - seeds[:, 1, :]
        offset = jnp.sum(seeds[:, 1, :] ** 2, axis=1) - jnp.sum(seeds[:, 0, :] ** 2, axis=1)
        chosen = (member_ids[level][:, None] == splits[None, :]).astype(jnp.float32)
        projected = lax.dot_general(embeddings, delta, (((1,), (1,)), ((), ())), precision=high)
        gap = jnp.sum(chosen * (2.0 * projected + offset[None, :]), axis=1)
        first = jax.nn.sigmoid(gap * scale)
        inside = jnp.sum(chosen, axis=1)
        weights_out.append(first * inside)
        weights = jnp.stack([chosen * first[:, None], chosen * (1.0 - first)[:, None]], axis=2)
        weights = weights.reshape(rows_dev, clusters)
        sums = lax.dot_general(weights, embeddings, (((0,), (0,)), ((), ())), precision=high)
        counts = jnp.sum(weights, axis=0)
        energy = jnp.dot(squares, weights, precision=high)
        seeds_flat = seeds.reshape(clusters, width)
        sums, counts, energy = lax.psum((sums, counts, energy), ("rows", "hosts"))
        current, spread = finish(sums, counts, energy, seeds_flat, width)
        spreads.append(spread)
    return (current, jnp.stack(spreads), jnp.stack(weights_out))


def solution(mesh):
    in_specs = (P(("rows", "hosts"), None), P(), P(None, ("rows", "hosts")), P(), P())
    out_specs = (P(), P(), P(None, ("rows", "hosts")))
    return jax.shard_map(
        on_device, mesh=mesh, in_specs=in_specs, out_specs=out_specs, check_vma=False
    )
```

profile of v0, /device:TPU:0, one launch (start us, length us, event | category | flops | bytes accessed | tf_op | source)
XLA Modules:
  0.0 662.1 jit_solution(14168517204198608662)
XLA Ops:
  9.5 5.1 gather_fusion.1
  20.8 5.1 gather_fusion.3
  34.2 120.2 %all-reduce.8.cloned.1.call-done = f32[256,2,768]{2,1,0:T(2,128)} async-done(((f32[256,2,768]{2,1,0:T(2,128)}), f32[256,2,768]{2,1,0:T(2,128)}) %all-reduce.8.cloned.1.call-update) | async-done | bytes 1572880 | tf_op jit(solution)/shard_map/psum | solution.py:33
  157.2 3.3 multiply_reduce_fusion.11
  165.2 3.3 fusion.26
  168.5 3.9 reshape.715
  172.4 9.0 %fusion.29 = f32[512,768]{1,0:T(8,128)} fusion(f32[1024,512]{0,1:T(8,128)} %reshape.715, f32[1024,768]{1,0:T(8,128)} %param.9), kind=kOutput, calls=%fused_computation.116 | convolution fusion | flops 4831838208 | bytes 6815744 | tf_op jit(solution)/shard_map/dot_general | solution.py:47
  182.1 5.1 gather_fusion.5
  192.9 39.8 %psum.86 = f32[512]{0:T(512)S(1)} all-reduce(f32[512]{0:T(512)S(1)} %reduce_sum.214), channel_id=1, replica_groups=mesh['rows'=8,'hosts'=4] {'rows','hosts'}, use_global_device_ids=true, to_apply=%region_6.9 | all-reduce | flops 512 | bytes 4096 | tf_op jit(solution)/shard_map/psum | solution.py:51
  232.7 86.2 %all-reduce.14.cloned.1.call-done = (f32[256,2,768]{2,1,0:T(2,128)}, f32[512,768]{1,0:T(8,128)}) async-done(((f32[256,2,768]{2,1,0:T(2,128)}, f32[512,768]{1,0:T(8,128)}), (f32[256,2,768]{2,1,0:T(2,128)}, f32[512,768]{1,0:T(8,128)})) %all-reduce.14.cloned.1.call-update) | async-done | bytes 3145744 | tf_op jit(solution)/shard_map/psum | solution.py:33
  324.2 3.3 multiply_reduce_fusion.9
  332.2 3.3 fusion.25
  335.5 3.8 reshape.717
  339.3 9.0 %fusion.30 = f32[512,768]{1,0:T(8,128)} fusion(f32[1024,512]{0,1:T(8,128)} %reshape.717, f32[1024,768]{1,0:T(8,128)} %param.9), kind=kOutput, calls=%fused_computation.117 | convolution fusion | flops 4831838208 | bytes 6815744 | tf_op jit(solution)/shard_map/dot_general | solution.py:47
  354.2 39.7 %psum.89 = f32[512]{0:T(512)S(1)} all-reduce(f32[512]{0:T(512)S(1)} %reduce_sum.219), channel_id=1, replica_groups=mesh['rows'=8,'hosts'=4] {'rows','hosts'}, use_global_device_ids=true, to_apply=%region_13.16 | all-reduce | flops 512 | bytes 4096 | tf_op jit(solution)/shard_map/psum | solution.py:51
  393.9 3.4 fusion.33
  397.4 88.8 %all-reduce.12.cloned.1.call-done = (f32[256,2,768]{2,1,0:T(2,128)}, f32[512,768]{1,0:T(8,128)}) async-done(((f32[256,2,768]{2,1,0:T(2,128)}, f32[512,768]{1,0:T(8,128)}), (f32[256,2,768]{2,1,0:T(2,128)}, f32[512,768]{1,0:T(8,128)})) %all-reduce.12.cloned.1.call-update) | async-done | bytes 3145744 | tf_op jit(solution)/shard_map/psum | solution.py:33
  491.5 4.0 multiply_reduce_fusion.7
  496.6 5.0 fusion.11
  506.8 4.0 reshape.719
  510.7 8.9 %fusion.31 = f32[512,768]{1,0:T(8,128)} fusion(f32[1024,512]{0,1:T(8,128)} %reshape.719, f32[1024,768]{1,0:T(8,128)} %param.9), kind=kOutput, calls=%fused_computation.118 | convolution fusion | flops 4831838208 | bytes 6815744 | tf_op jit(solution)/shard_map/dot_general | solution.py:47
  519.7 3.4 fusion.34
  523.0 39.4 %all-reduce = (f32[512]{0:T(512)S(1)}, f32[512]{0:T(512)S(1)}, f32[512]{0:T(512)S(1)}, f32[512]{0:T(512)S(1)}) all-reduce(f32[512]{0:T(512)S(1)} %reduce_sum.224, f32[512]{0:T(512)S(1)} %bitcast.113, f32[512]{0:T(512)S(1)} %bitcast.112, f32[512]{0:T(512)S(1)} %bitcast.111), channel_id=1, replica_groups=mesh['rows'=8,'hosts'=4] {'rows','hosts'}, use_global_device_ids=true, to_apply=%region_20.23 | all-reduce | flops 2048 | bytes 16384 | tf_op jit(solution)/shard_map/psum | solution.py:51
  563.1 88.7 %all-reduce.10.cloned.1.call-done = f32[512,768]{1,0:T(8,128)} async-done(((f32[512,768]{1,0:T(8,128)}), f32[512,768]{1,0:T(8,128)}) %all-reduce.10.cloned.1.call-update) | async-done | bytes 1572880 | tf_op jit(solution)/shard_map/psum | solution.py:51
  (100 shorter events, 62.0 us)
Async XLA Ops:
  7.2 20.9 %copy-start = (f32[512,768]{1,0:T(8,128)S(1)}, f32[512,768]{1,0:T(8,128)}, u32[]{:S(2)}) copy-start(f32[512,768]{1,0:T(8,128)} %param.10) | copy-start | bytes 4718596
  7.2 147.3 %all-reduce.8.cloned.1.call-start = ((), (), s32[]{:S(2)}) async-start(), calls=%async_computation | async-start | bytes 3145728 | tf_op jit(solution)/shard_map/psum | solution.py:33
  18.8 1.1 copy-start.7
  18.8 300.0 %all-reduce.14.cloned.1.call-start = ((), (), s32[]{:S(2)}) async-start(), calls=%async_computation.3 | async-start | bytes 6291456 | tf_op jit(solution)/shard_map/psum | solution.py:33
  154.4 6.1 copy-start.2
  181.4 304.8 %all-reduce.12.cloned.1.call-start = ((), (), s32[]{:S(2)}) async-start(), calls=%async_computation.2 | async-start | bytes 6291456 | tf_op jit(solution)/shard_map/psum | solution.py:33
  321.8 1.4 copy-start.5
  323.2 4.3 copy-start.3
  348.3 303.4 %all-reduce.10.cloned.1.call-start = ((), (), s32[]{:S(2)}) async-start(), calls=%async_computation.1 | async-start | bytes 3145728 | tf_op jit(solution)/shard_map/psum | solution.py:51
  348.6 2.5 copy-start.4
  489.1 1.4 copy-start.6
  563.1 92.1 %copy-start.1 = (f32[512,768]{1,0:T(8,128)S(1)}, f32[512,768]{1,0:T(8,128)}, u32[]{:S(2)}) copy-start(f32[512,768]{1,0:T(8,128)} %param.10) | copy-start | bytes 4718596
Sparse Core Ops, SparseCore 0:
  19.0 135.4 all-reduce.7
  181.5 137.2 all-reduce.13
  348.5 137.6 all-reduce.11
  519.8 131.9 all-reduce.9
where the time goes:
time: 666 us; the launch traced here: 662 us
  waiting for transfers between devices  384 us (58%)
  blocking collectives  119 us (18%)
  other arithmetic  51.2 us (8%)
  local copies, waits for them, and re-layouts  46.9 us (7%)
  matrix products  46.3 us (7%)
  between operations  14.5 us (2%)
    psum x3, waiting for transfers between devices, on_device(): lax.psum(jnp.where(inside[..., None], picked, jnp.float32(0.0)), ('rows',...  295 us
    psum x3, blocking collectives, on_device(): sums, counts, energy = lax.psum((sums, counts, energy), ('rows', 'hosts'))  119 us
    psum x1, waiting for transfers between devices, on_device(): sums, counts, energy = lax.psum((sums, counts, energy), ('rows', 'hosts'))  88.7 us
    dot_general x3, matrix products, on_device(): lax.dot_general(weights, embeddings, (((0,), (0,)), ((), ())), precision=...  26.9 us
    gather x6, local copies, waits for them, and re-layouts, on_device(): picked = jnp.take(embeddings, jnp.clip(local, 0, rows_dev - 1), axis=0)  21.9 us
  transfers between devices with their start and end apart: 4, of which 4 were waited for; matrix products, arithmetic and copies ran while one was open for 6% of the time, Pallas kernels for 0%

commit v1 on v0

v1 whole, which is shorter than its diff:
```python
import functools

import jax
import jax.numpy as jnp
from jax import lax
from jax.experimental import pallas as pl
from jax.experimental.pallas import tpu as pltpu
from jax.sharding import PartitionSpec as P

AXES = ("rows", "hosts")
LANES = 128
F32 = jnp.float32
BF16 = jnp.bfloat16


class Comm:
    def __init__(self, devices, most_blocks):
        self.n = devices
        self.me = lax.axis_index(AXES)
        bits = devices.bit_length() - 1
        assert 1 << bits == devices
        radices = [2] * (bits % 2) + [4] * (bits // 2)
        self.stages, self.extra = [], []
        self.blocks, stride, self.block = 1, 1, 0
        for radix in radices:
            if self.blocks * radix <= most_blocks:
                self.stages.append((radix, stride))
                self.block = self.block * radix + (self.me // stride) % radix
                self.blocks *= radix
            else:
                self.extra.append((radix, stride))
            stride *= radix
        self.lead = self.stages[0][0]

    def send(self, x, mask):
        return lax.ppermute(x, AXES, [(i, i ^ mask) for i in range(self.n)])

    def reduce_scatter(self, pieces):
        for step, (radix, stride) in enumerate(self.stages):
            if step:
                x = x.reshape((radix, x.shape[0] // radix) + x.shape[1:])
                pieces = [x[j] for j in range(radix)]
            got = [self.send(pieces[j], j * stride) for j in range(1, radix)]
            x = functools.reduce(jnp.add, got, pieces[0])
        x = x[0]
        for radix, stride in self.extra:
            while radix > 1:
                x = x + self.send(x, stride)
                stride, radix = stride * 2, radix // 2
        return x

    def all_gather(self, x):
        x = x[None]
        for radix, stride in self.stages[::-1]:
            pieces = [x] + [self.send(x, j * stride) for j in range(1, radix)]
            if (radix, stride) != self.stages[0]:
                x = jnp.concatenate(pieces)
        return pieces

    def share(self, x):
        return lax.all_to_all(x, AXES, 0, 0, tiled=True)


def dot(a, b):
    return lax.dot_general(a, b, (((1,), (0,)), ((), ())), preferred_element_type=F32)


def dot_t(a, b):
    return lax.dot_general(a, b, (((1,), (1,)), ((), ())), preferred_element_type=F32)


def split2(x):
    high = x.astype(BF16)
    return high, (x - high.astype(F32)).astype(BF16)


def iota(shape, axis):
    return lax.broadcasted_iota(jnp.int32, shape, axis)


def lane_sum(x):
    return jnp.sum(x, axis=1, keepdims=True)


def pack(columns):
    rows = columns[0].shape[0]
    lane = iota((rows, LANES), 1)
    out = jnp.zeros((rows, LANES), F32)
    for q, c in enumerate(columns):
        out = jnp.where(lane == q, c, out)
    return out


def to_blocks(scratch, outs, block, own, per):
    for j, out in enumerate(outs):
        for t in range(per):
            at = (block ^ (j * per + t)) * own
            out[t] = scratch[pl.ds(pl.multiple_of(at, 8), own), :]


def from_blocks(pieces, scratch, block, own, per):
    for j, piece in enumerate(pieces):
        for t in range(per):
            at = (block ^ (j * per + t)) * own
            scratch[pl.ds(pl.multiple_of(at, 8), own), :] = piece[t]


def pick_kernel(place, seeds, emb, *refs, levels, lead, per, own):
    outs = refs[:lead]
    high, low, delta, mean, scratch = refs[lead:]
    rows, width = emb.shape
    splits = seeds.shape[1]
    e = emb[...]
    a = e.astype(BF16)
    rest = e - a.astype(F32)
    b = rest.astype(BF16)
    c = (rest - b.astype(F32)).astype(BF16)
    high[...] = a
    low[...] = b
    row = iota((splits, rows), 1) + place[1]
    bs = []
    for l in range(levels):
        hot0 = jnp.where(seeds[l, :, 0:1] == row, 0.5, 0.0)
        hot1 = jnp.where(seeds[l, :, 1:2] == row, 0.5, 0.0)
        d = (hot0 - hot1).astype(BF16)
        m = (hot0 + hot1).astype(BF16)
        dv = dot(d, a) + (dot(d, b) + dot(d, c))
        mv = dot(m, a) + (dot(m, b) + dot(m, c))
        delta[l] = dv
        mean[l] = mv
        scratch[:, l * width : (l + 1) * width] = dv
        bs.append(lane_sum(dv * mv))
    scratch[:, levels * width :] = pack(bs)
    to_blocks(scratch, outs, place[0], own, per)


def level_step(l, levels, offset, proj, cols, member, sq, rows_in, lookups, scale):
    splits, rows = proj.shape[1:]
    chosen = cols[:, l : l + 1] == member[l : l + 1, :]
    part = jnp.where(chosen, proj[l] - offset, 0.0)
    gap = 2.0 * jnp.sum(part, axis=0, keepdims=True)
    inside = jnp.sum(jnp.where(chosen, 1.0, 0.0), axis=0, keepdims=True)
    first = jax.nn.sigmoid(gap * scale)
    number = iota((splits, rows), 0).astype(F32)
    index = jnp.sum(jnp.where(chosen, number + 1.0, 0.0), axis=0, keepdims=True) - 1.0
    w0 = jnp.where(chosen, first, 0.0)
    w1 = jnp.where(chosen, 1.0 - first, 0.0)
    columns = [lane_sum(w0), lane_sum(w1), lane_sum(w0 * sq), lane_sum(w1 * sq)]
    rows_out = rows_in + [(index, first)]
    if l + 1 < levels:
        row = iota((splits, rows), 1)
        coef = jnp.ones((splits, 1), F32)
        total = jnp.zeros((splits, 1), F32)
        for k in range(l, -1, -1):
            half, odd, seed = ancestor(cols, levels, l + 1, k)
            if k < l:
                coef = coef * lookups[k](half, odd)
            at, f = rows_out[k]
            w = jnp.where(at == half.astype(F32), jnp.where(odd > 0, 1.0 - f, f), 0.0)
            w = w + jnp.where(row == seed, 0.5, 0.0)
            total = total + coef * lane_sum(w * proj[l + 1])
            coef = 0.5 * coef
        columns += [total, coef]
    return first * inside, rows_out, columns


def ancestor(cols, levels, l, k):
    at = 2 * levels + 3 * (l * (l - 1) // 2 + k)
    return cols[:, at : at + 1], cols[:, at + 1 : at + 2], cols[:, at + 2 : at + 3]


def emit(columns, small, shared, n):
    packed = pack(columns)
    small[...] = packed
    across = jnp.transpose(packed)[:8, :]
    for i in range(n):
        shared[i] = across


def project_kernel(place, *refs, levels, lead, per, own, n, scale):
    pieces = refs[:lead]
    high, low, emb, root, cols, member = refs[lead : lead + 6]
    proj, stat, small, shared, state, out, scratch = refs[lead + 6 :]
    rows, width = emb.shape
    splits = proj.shape[1]
    from_blocks(pieces, scratch, place[0], own, per)
    e = emb[...]
    q = e * e
    ones = jnp.ones((8, width), BF16)
    qa = q.astype(BF16)
    rest = q - qa.astype(F32)
    qb = rest.astype(BF16)
    qc = (rest - qb.astype(F32)).astype(BF16)
    sq = (dot_t(ones, qa) + (dot_t(ones, qb) + dot_t(ones, qc)))[0:1, :]
    a, b = high[...], low[...]
    ra, rb = split2(root[...])
    lane = iota((splits, root.shape[0]), 1)
    stats = [scratch[:, levels * width + l : levels * width + l + 1] for l in range(levels)]
    for l in range(levels):
        da, db = split2(scratch[:, l * width : (l + 1) * width])
        proj[l] = dot_t(da, a) + (dot_t(da, b) + dot_t(db, a))
        g = dot_t(da, ra) + (dot_t(da, rb) + dot_t(db, ra))
        at = cols[:, levels + l : levels + l + 1]
        stats.append(lane_sum(jnp.where(lane == at, g, 0.0)))
    stat[...] = pack(stats)
    offset = 0.5 * (stats[levels] + stats[0])
    weight, kept, columns = level_step(
        0, levels, offset, proj, cols, member, sq, [], [], scale
    )
    out[...] = weight
    state[...] = jnp.zeros(state.shape, F32)
    state[0:1, :] = sq
    state[1:2, :] = kept[0][0]
    state[2:3, :] = kept[0][1]
    emit(columns, small, shared, n)


def level_kernel(got, proj, stat, before, counts, state, cols, member, *refs, l, levels, n, scale):
    small, shared, state_out, counts_out, out = refs
    splits = proj.shape[1]
    total = got[0]
    for i in range(1, n):
        total = total + got[i]
    fill = jnp.zeros((LANES - 8, splits), F32)
    down = jnp.transpose(jnp.concatenate([total, fill], axis=0))
    counts_out[...] = counts[...]
    counts_out[2 * (l - 1) : 2 * l, :] = 1.0 / (total[0:2, :] + 1.0)
    lane = iota((splits, splits), 1)

    def lookup(k):
        def run(half, odd):
            value = jnp.where(
                odd > 0, counts_out[2 * k + 1 : 2 * k + 2, :], counts_out[2 * k : 2 * k + 1, :]
            )
            return lane_sum(jnp.where(lane == half, value, 0.0))

        return run

    lookups = [lookup(k) for k in range(l)]
    half, odd, _ = ancestor(cols, levels, l, l - 1)
    inverse = lookups[l - 1](half, odd)
    root = stat[:, levels + l : levels + l + 1]
    dots = (down[:, 4:5] + before[:, 5:6] * root) * inverse
    offset = 0.5 * (dots + stat[:, l : l + 1])
    kept = [(state[1 + 2 * k : 2 + 2 * k, :], state[2 + 2 * k : 3 + 2 * k, :]) for k in range(l)]
    weight, kept, columns = level_step(
        l, levels, offset, proj, cols, member, state[0:1, :], kept, lookups, scale
    )
    out[...] = weight
    state_out[...] = state[...]
    state_out[1 + 2 * l : 2 + 2 * l, :] = kept[l][0]
    state_out[2 + 2 * l : 3 + 2 * l, :] = kept[l][1]
    columns = columns + [jnp.zeros((splits, 1), F32)] * (6 - len(columns)) + [inverse]
    emit(columns, small, shared, n)


def sums_kernel(place, nodes, *refs, l, levels, lead, per, own, clusters_rows):
    high, low, delta, mean, state, cols, small, before = refs[:8]
    outs = refs[8 : 8 + lead]
    total, scratch = refs[8 + lead :]
    rows, width = high.shape
    splits = delta.shape[1]
    number = iota((splits, rows), 0).astype(F32)
    index = state[1 + 2 * l : 2 + 2 * l, :]
    first = state[2 + 2 * l : 3 + 2 * l, :]
    chosen = number == index
    a, b = high[...], low[...]
    for j, f in enumerate((first, 1.0 - first)):
        wa, wb = split2(jnp.where(chosen, f, 0.0))
        scratch[:, j * width : (j + 1) * width] = dot(wa, a) + (dot(wa, b) + dot(wb, a))
    at = slice(2 * width, 3 * width)

    def move(s, carry):
        node = nodes[s]
        if l:
            value = before[lax.rem(node, 2), pl.ds(lax.div(node, 2), 1), :]
        else:
            value = before[pl.ds(node, 1), :]
        scratch[pl.ds(s, 1), at] = value
        return carry

    lax.fori_loop(0, splits, move, 0, unroll=8)
    if l:
        factor = small[:, 6:7]
    else:
        factor = jnp.where(place[2] == 0, 1.0, 0.0)
    mid = 0.5 * (scratch[:, at] * factor + mean[l])
    scratch[:, at] = mid
    half = 0.5 * delta[l]
    total[0] = scratch[:, 0:width] + (mid + half)
    total[1] = scratch[:, width : 2 * width] + (mid - half)
    scratch[:, 3 * width :] = small[...]
    to_blocks(scratch, outs, place[0], own, per)


def finish_kernel(*refs, levels):
    sums = refs[:levels]
    delta, out = refs[levels:]
    own = out.shape[0] // 2
    width = out.shape[1] - LANES
    spread = []
    for l in range(levels):
        mid = sums[l][:, 2 * width : 3 * width]
        half = 0.5 * delta[:, l * width : (l + 1) * width]
        for j in range(2):
            s = sums[l][:, j * width : (j + 1) * width]
            count = sums[l][:, 3 * width + j : 3 * width + j + 1]
            energy = sums[l][:, 3 * width + 2 + j : 3 * width + 3 + j]
            centre = (s + (mid + half if j == 0 else mid - half)) / (count + 1.0)
            error = (
                energy - 2.0 * lane_sum(centre * s) + count * lane_sum(centre * centre)
            )
            spread.append(error / ((count + 1.0) * width))
            if l + 1 == levels:
                for i in range(own):
                    out[2 * i + j : 2 * i + j + 1, :width] = centre[i : i + 1, :]
    out[:own, width:] = pack(spread)
    out[own:, width:] = jnp.zeros((own, LANES), F32)


def place_kernel(place, *refs, levels, lead, per, own):
    pieces = refs[:lead]
    centre, spread, scratch = refs[lead:]
    splits, width = scratch.shape[0], centre.shape[1]
    for j, piece in enumerate(pieces):
        for t in range(per):
            at = (place[0] ^ (j * per + t)) * own
            centre[pl.ds(pl.multiple_of(2 * at, 8), 2 * own), :] = piece[t, :, :width]
            scratch[pl.ds(pl.multiple_of(at, 8), own), :] = piece[t, :own, width:]
    across = jnp.transpose(scratch[...])[:8, :]
    a = across.astype(BF16)
    rest = across - a.astype(F32)
    b = rest.astype(BF16)
    c = (rest - b.astype(F32)).astype(BF16)
    total = jnp.zeros((8, 2 * splits), F32)
    outs = []
    for j in range(2):
        hot = jnp.where(
            iota((splits, 2 * splits), 1) == 2 * iota((splits, 2 * splits), 0) + j, 1.0, 0.0
        ).astype(BF16)
        outs.append(dot(a, hot) + (dot(b, hot) + dot(c, hot)))
    for l in range(levels):
        spread[l : l + 1, :] = outs[0][2 * l : 2 * l + 1, :] + outs[1][2 * l + 1 : 2 * l + 2, :]


def on_device(embeddings, root_centroids, member_ids, split_order, seed_rows):
    rows, width = embeddings.shape
    levels, splits = seed_rows.shape[:2]
    comm = Comm(lax.axis_size(AXES), splits // 8)
    n, lead = comm.n, comm.lead
    own = splits // comm.blocks
    per = comm.blocks // lead
    payload = levels * width + LANES
    scale = 0.5 / (float(width) ** 0.5)
    first_row = comm.me * rows
    place = jnp.stack([comm.block, first_row, comm.me]).astype(jnp.int32)
    smem = pl.BlockSpec(memory_space=pltpu.SMEM)
    vmem = pl.BlockSpec(memory_space=pltpu.VMEM)
    piece = jax.ShapeDtypeStruct((per, own, payload), F32)
    geometry = dict(lead=lead, per=per, own=own)

    def struct(shape, dtype=F32):
        return jax.ShapeDtypeStruct(shape, dtype)

    def call(kernel, name, outs, scalars, args, scratch=()):
        return pl.pallas_call(
            kernel,
            name=name,
            out_shape=outs,
            in_specs=[smem] * len(scalars) + [vmem] * len(args),
            out_specs=[vmem] * len(outs),
            scratch_shapes=[pltpu.VMEM(s, F32) for s in scratch],
            compiler_params=pltpu.CompilerParams(vmem_limit_bytes=60 * 1024 * 1024),
        )(*scalars, *args)

    *sent, high, low, delta, mean = call(
        functools.partial(pick_kernel, levels=levels, **geometry),
        "pick",
        [piece] * lead
        + [struct((rows, width), BF16)] * 2
        + [struct((levels, splits, width))] * 2,
        [place],
        [seed_rows, embeddings],
        [(splits, payload)],
    )

    order = split_order[:, :splits]
    local = seed_rows.reshape(levels, 2 * splits) - first_row
    chain, root_at = [], []
    for l in range(levels):
        node = order[l]
        found = []
        for k in range(l - 1, -1, -1):
            found.append([node // 2, node % 2, jnp.take(local[k], node)])
            node = jnp.take(order[k], node // 2)
        root_at.append(node)
        for entry in found[::-1]:
            chain += entry
    cols = jnp.stack([order[l] for l in range(levels)] + root_at + chain, axis=1)

    delta_own = comm.reduce_scatter(sent)
    pieces = comm.all_gather(delta_own)
    proj, stat, small, shared, state, weight = call(
        functools.partial(
            project_kernel, levels=levels, n=n, scale=scale, **geometry
        ),
        "project",
        [
            struct((levels, splits, rows)),
            struct((splits, LANES)),
            struct((splits, LANES)),
            struct((n, 8, splits)),
            struct((8, rows)),
            struct((1, rows)),
        ],
        [place],
        [*pieces, high, low, embeddings, root_centroids, cols, member_ids],
        [(splits, payload)],
    )
    weights_out = [weight]
    counts = jnp.zeros((8, splits), F32)
    before = root_centroids
    sums_own = []
    for l in range(levels):
        if l:
            got = comm.share(shared)
            small, shared, state, counts, weight = call(
                functools.partial(level_kernel, l=l, levels=levels, n=n, scale=scale),
                f"level{l}",
                [
                    struct((splits, LANES)),
                    struct((n, 8, splits)),
                    struct((8, rows)),
                    struct((8, splits)),
                    struct((1, rows)),
                ],
                [],
                [got, proj, stat, small, counts, state, cols, member_ids],
            )
            weights_out.append(weight)
        *sent, before = call(
            functools.partial(
                sums_kernel, l=l, levels=levels, clusters_rows=2 * splits, **geometry
            ),
            f"sums{l}",
            [piece] * lead + [struct((2, splits, width))],
            [place, order[l]],
            [high, low, delta, mean, state, cols, small, before],
            [(splits, payload)],
        )
        sums_own.append(comm.reduce_scatter(sent))
    (final,) = call(
        functools.partial(finish_kernel, levels=levels),
        "finish",
        [struct((2 * own, width + LANES))],
        [],
        [*sums_own, delta_own],
    )
    pieces = comm.all_gather(final)
    centre, spread = call(
        functools.partial(place_kernel, levels=levels, **geometry),
        "place",
        [struct((2 * splits, width)), struct((levels, 2 * splits))],
        [place],
        pieces,
        [(splits, LANES)],
    )
    return (centre, spread, jnp.concatenate(weights_out, axis=0))


def solution(mesh):
    in_specs = (P(AXES, None), P(), P(None, AXES), P(), P())
    out_specs = (P(), P(), P(None, AXES))
    return jax.shard_map(
        on_device, mesh=mesh, in_specs=in_specs, out_specs=out_specs, check_vma=False
    )
```

time: 666 us -> 240 us (0.36)
  waiting for transfers between devices: 384 us -> 68.5 us
  blocking collectives: 119 us -> 12.9 us
  Pallas kernels: 0 us -> 72.1 us
  starting transfers between devices: 0.34 us -> 52.4 us
  matrix products: 46.3 us -> 0 us
  other arithmetic: 51.2 us -> 9.93 us
  local copies, waits for them, and re-layouts: 46.9 us -> 22.4 us
  between operations: 14.5 us -> 1.28 us
    psum x4 -> x0, waiting for transfers between devices: 384 us -> none  [the longest x3 295 us: on_device(): lax.psum(jnp.where(inside[..., None], picked, jnp.float32(0.0)), ('rows',...]
    psum x3 -> x0, blocking collectives: 119 us -> none  [on_device(): sums, counts, energy = lax.psum((sums, counts, energy), ('rows', 'hosts'))]
    pallas_call x0 -> x9, Pallas kernels: none -> 72.1 us  [call(): pl.pallas_call(kernel, name=name, out_shape=outs, in_specs=[smem] * len(s...]
    ppermute x0 -> x42, waiting for transfers between devices: none -> 68.5 us  [send(): return lax.ppermute(x, AXES, [(i, i ^ mask) for i in range(self.n)])]
    ppermute x0 -> x42, starting transfers between devices: none -> 49.6 us  [send(): return lax.ppermute(x, AXES, [(i, i ^ mask) for i in range(self.n)])]
    dot_general x9 -> x0, matrix products: 46.3 us -> none  [the longest x3 26.9 us: on_device(): lax.dot_general(weights, embeddings, (((0,), (0,)), ((), ())), precision=...]
    reduce_sum x13 -> x0, other arithmetic: 29.9 us -> none  [the longest x3 10.6 us: on_device(): jnp.sum(seeds[:, 0, :] ** 2, axis=1)]
    reshape x6 -> x0, local copies, waits for them, and re-layouts: 14.9 us -> none  [the longest x3 11.7 us: on_device(): weights = weights.reshape(rows_dev, clusters)]
  transfers between devices with their start and end apart: 4 -> 43, of which waited for: 4 -> 26; matrix products, arithmetic and copies ran while one was open for 6% -> 9% of each run, Pallas kernels for 0% -> 13%
where the time goes in v1:
time: 240 us
  Pallas kernels  72.1 us (30%)
  waiting for transfers between devices  68.5 us (29%)
  starting transfers between devices  52.4 us (22%)
  local copies, waits for them, and re-layouts  22.4 us (9%)
  blocking collectives  12.9 us (5%)
  other arithmetic  9.93 us (4%)
    pallas_call x9, Pallas kernels, call(): pl.pallas_call(kernel, name=name, out_shape=outs, in_specs=[smem] * len(s...  72.1 us
    ppermute x42, waiting for transfers between devices, send(): return lax.ppermute(x, AXES, [(i, i ^ mask) for i in range(self.n)])  68.5 us
    ppermute x42, starting transfers between devices, send(): return lax.ppermute(x, AXES, [(i, i ^ mask) for i in range(self.n)])  49.6 us
    all_to_all x1, blocking collectives, share(): return lax.all_to_all(x, AXES, 0, 0, tiled=True)  12.9 us
    unnamed x54, local copies, waits for them, and re-layouts  7.49 us
    gather x3, local copies, waits for them, and re-layouts, on_device(): node = jnp.take(order[k], node // 2)  6.01 us
    gather x3, local copies, waits for them, and re-layouts, on_device(): found.append([node // 2, node % 2, jnp.take(local[k], node)])  5.83 us
    add x8, other arithmetic, reduce_scatter(): x = functools.reduce(jnp.add, got, pieces[0])  5.57 us
  transfers between devices with their start and end apart: 43, of which 26 were waited for; matrix products, arithmetic and copies ran while one was open for 9% of the time, Pallas kernels for 13%

profile of v1, /device:TPU:0, one launch (start us, length us, event | category | flops | bytes accessed | tf_op | source)
XLA Modules:
  0.0 239.6 jit_solution(9230396482212000172)
XLA Ops:
  2.9 13.6 %pick.1 = (f32[16,8,2432]{2,1,0:T(8,128)}, f32[16,8,2432]{2,1,0:T(8,128)}, bf16[1024,768]{1,0:T(8,128)(2,1)}, bf16[1024,768]{1,0:T(8,128)(2,1)}, f32[3,256,768]{2,1,0:T(8,128)}, /*index=5*/f32[3,256,768]{2,1,0:T(8,128)}) custom-call(s32[3]{0:T(128)} %pad_add_fusion.place, s32[3,256,2]{2,1,0:T(8,128)} %copy.31.seeds, f32[1024,768]{1,0:T(8,128)} %refs_4_.1), custom_call_target="tpu_custom_call" | custom-call | tf_op jit(solution)/shard_map/pick/pallas_call | solution.py:366
  22.4 2.9 %collective-permute-start.1 = (f32[4,8,2432]{2,1,0:T(8,128)S(1)}, f32[4,8,2432]{2,1,0:T(8,128)S(1)}, u32[]{:S(2)}, u32[]{:S(2)}) collective-permute-start(f32[4,8,2432]{2,1,0:T(8,128)S(1)} %get-tuple-element.84), channel_id=1, source_target_pairs={{0,2},{1,3},{2,0},{3,1},{4,6},{5,7},{6,4},{7,5},{8,10},{9,11},{10,... | collective-permute-start | bytes 933896 | tf_op jit(solution)/shard_map/ppermute | solution.py:36
  29.1 4.4 %collective-permute-done.1 = f32[4,8,2432]{2,1,0:T(8,128)S(1)} collective-permute-done((f32[4,8,2432]{2,1,0:T(8,128)S(1)}, f32[4,8,2432]{2,1,0:T(8,128)S(1)}, u32[]{:S(2)}, u32[]{:S(2)}) %collective-permute-start.1) | collective-permute-done | bytes 311328 | tf_op jit(solution)/shard_map/ppermute | solution.py:36
  33.5 7.4 %collective-permute-done.3 = f32[4,8,2432]{2,1,0:T(8,128)S(1)} collective-permute-done((f32[4,8,2432]{2,1,0:T(8,128)S(1)}, f32[4,8,2432]{2,1,0:T(8,128)S(1)}, u32[]{:S(2)}, u32[]{:S(2)}) %collective-permute-start.3) | collective-permute-done | bytes 311328 | tf_op jit(solution)/shard_map/ppermute | solution.py:36
  51.4 2.9 %collective-permute-done.5 = f32[1,8,2432]{2,1,0:T(8,128)S(1)} collective-permute-done((f32[1,8,2432]{2,1,0:T(8,128)S(1)}, f32[1,8,2432]{2,1,0:T(8,128)S(1)}, u32[]{:S(2)}, u32[]{:S(2)}) %collective-permute-start.5) | collective-permute-done | bytes 77856 | tf_op jit(solution)/shard_map/ppermute | solution.py:36
  65.9 8.4 %collective-permute-done.10 = f32[4,8,2432]{2,1,0:T(8,128)S(1)} collective-permute-done((f32[4,8,2432]{2,1,0:T(8,128)S(1)}, f32[4,8,2432]{2,1,0:T(8,128)S(1)}, u32[]{:S(2)}, u32[]{:S(2)}) %collective-permute-start.10) | collective-permute-done | bytes 311328 | tf_op jit(solution)/shard_map/ppermute | solution.py:36
  83.5 13.1 %project.1 = (f32[3,256,1024]{2,1,0:T(8,128)}, f32[256,128]{1,0:T(8,128)}, f32[256,128]{1,0:T(8,128)}, f32[32,8,256]{2,1,0:T(8,128)}, f32[8,1024]{1,0:T(8,128)}, /*index=5*/f32[1,1024]{1,0:T(1,128)}) custom-call(s32[3]{0:T(128)} %pad_add_fusion.place, f32[16,8,2432]{2,1,0:T(8,128)} %copy-done.2, f32[16,8,2432]{2,1,0:T(8,128)} %copy-done.9, ...), custom_call_target="tpu_custom_call" | custom-call | tf_op jit(solution)/shard_map/project/pallas_call | solution.py:366
  96.5 9.9 %sums0.1 = (f32[16,8,2432]{2,1,0:T(8,128)}, f32[16,8,2432]{2,1,0:T(8,128)}, f32[2,256,768]{2,1,0:T(8,128)}) custom-call(s32[3]{0:T(128)} %pad_add_fusion.place, s32[256]{0:T(256)} %bitcast.36, bf16[1024,768]{1,0:T(8,128)(2,1)} %get-tuple-element.35.refs_2_.refs_0_, bf16[1024,768]{1,0:T(8,128)(2,1)} %get-tuple-element.36.refs_3_.refs_1_, ...), custom_call_target="tpu_custom_call" | custom-call | tf_op jit(solution)/shard_map/sums0/pallas_call | solution.py:366
  106.9 12.9 %all_to_all.10.got = f32[32,8,256]{2,1,0:T(8,128)} all-to-all(f32[32,8,256]{2,1,0:T(8,128)S(1)} %copy-done.14), channel_id=1, replica_groups=mesh['rows'=8,'hosts'=4] {'rows','hosts'}, dimensions={0} | all-to-all | bytes 524288 | tf_op jit(solution)/shard_map/all_to_all | solution.py:61
  120.5 5.3 %level1.1 = (f32[256,128]{1,0:T(8,128)}, f32[32,8,256]{2,1,0:T(8,128)}, f32[8,1024]{1,0:T(8,128)}, f32[8,256]{1,0:T(8,128)}, f32[1,1024]{1,0:T(1,128)}) custom-call(f32[32,8,256]{2,1,0:T(8,128)} %all_to_all.10.got, f32[3,256,1024]{2,1,0:T(8,128)} %get-tuple-element.46.proj, f32[256,128]{1,0:T(8,128)} %get-tuple-element.47.stat, ...), custom_call_target="tpu_custom_call" | custom-call | tf_op jit(solution)/shard_map/level1/pallas_call | solution.py:366
  125.8 2.8 %all-to-all-start.1 = ((f32[32,8,256]{2,1,0:T(8,128)}), f32[32,8,256]{2,1,0:T(8,128)S(1)}, u32[]{:S(2)}, u32[]{:S(2)}) async-start(f32[32,8,256]{2,1,0:T(8,128)} %get-tuple-element.53), calls=%async_computation.1 | async-start | bytes 524288 | tf_op jit(solution)/shard_map/all_to_all | solution.py:61
  135.4 10.8 %sums1.1 = (f32[16,8,2432]{2,1,0:T(8,128)}, f32[16,8,2432]{2,1,0:T(8,128)}, f32[2,256,768]{2,1,0:T(8,128)}) custom-call(s32[3]{0:T(128)} %pad_add_fusion.place, s32[256]{0:T(256)} %bitcast.40, bf16[1024,768]{1,0:T(8,128)(2,1)} %get-tuple-element.35.refs_2_.refs_0_, bf16[1024,768]{1,0:T(8,128)(2,1)} %get-tuple-element.36.refs_3_.refs_1_, ...), custom_call_target="tpu_custom_call" | custom-call | tf_op jit(solution)/shard_map/sums1/pallas_call | solution.py:366
  146.9 4.1 %level2.1 = (f32[256,128]{1,0:T(8,128)}, f32[32,8,256]{2,1,0:T(8,128)}, f32[8,1024]{1,0:T(8,128)}, f32[8,256]{1,0:T(8,128)}, f32[1,1024]{1,0:T(1,128)}) custom-call(f32[32,8,256]{2,1,0:T(8,128)} %copy-done.10, f32[3,256,1024]{2,1,0:T(8,128)} %get-tuple-element.46.proj, f32[256,128]{1,0:T(8,128)} %get-tuple-element.47.stat, ...), custom_call_target="tpu_custom_call" | custom-call | tf_op jit(solution)/shard_map/level2/pallas_call | solution.py:366
  150.9 10.7 %sums2.1 = (f32[16,8,2432]{2,1,0:T(8,128)}, f32[16,8,2432]{2,1,0:T(8,128)}, f32[2,256,768]{2,1,0:T(8,128)}) custom-call(s32[3]{0:T(128)} %pad_add_fusion.place, s32[256]{0:T(256)} %bitcast.48, bf16[1024,768]{1,0:T(8,128)(2,1)} %get-tuple-element.35.refs_2_.refs_0_, bf16[1024,768]{1,0:T(8,128)(2,1)} %get-tuple-element.36.refs_3_.refs_1_, ...), custom_call_target="tpu_custom_call" | custom-call | tf_op jit(solution)/shard_map/sums2/pallas_call | solution.py:366
  178.0 6.3 %collective-permute-done.24 = f32[4,8,2432]{2,1,0:T(8,128)S(1)} collective-permute-done((f32[4,8,2432]{2,1,0:T(8,128)S(1)}, f32[4,8,2432]{2,1,0:T(8,128)S(1)}, u32[]{:S(2)}, u32[]{:S(2)}) %collective-permute-start.24) | collective-permute-done | bytes 311328 | tf_op jit(solution)/shard_map/ppermute | solution.py:36
  184.3 2.6 %collective-permute-done.23 = f32[4,8,2432]{2,1,0:T(8,128)S(1)} collective-permute-done((f32[4,8,2432]{2,1,0:T(8,128)S(1)}, f32[4,8,2432]{2,1,0:T(8,128)S(1)}, u32[]{:S(2)}, u32[]{:S(2)}) %collective-permute-start.23) | collective-permute-done | bytes 311328 | tf_op jit(solution)/shard_map/ppermute | solution.py:36
  191.3 2.9 %collective-permute-start.27 = (f32[1,8,2432]{2,1,0:T(8,128)S(1)}, f32[1,8,2432]{2,1,0:T(8,128)S(1)}, u32[]{:S(2)}, u32[]{:S(2)}) collective-permute-start(f32[1,8,2432]{2,1,0:T(8,128)S(1)} %get-tuple-element.91), channel_id=1, source_target_pairs={{0,24},{1,25},{2,26},{3,27},{4,28},{5,29},{6,30},{7,31},{8,16},{9,... | collective-permute-start | bytes 233480 | tf_op jit(solution)/shard_map/ppermute | solution.py:36
  194.3 3.2 %collective-permute-done.29 = f32[4,8,2432]{2,1,0:T(8,128)S(1)} collective-permute-done((f32[4,8,2432]{2,1,0:T(8,128)S(1)}, f32[4,8,2432]{2,1,0:T(8,128)S(1)}, u32[]{:S(2)}, u32[]{:S(2)}) %collective-permute-start.29) | collective-permute-done | bytes 311328 | tf_op jit(solution)/shard_map/ppermute | solution.py:36
  198.2 4.3 %collective-permute-done.31 = f32[4,8,2432]{2,1,0:T(8,128)S(1)} collective-permute-done((f32[4,8,2432]{2,1,0:T(8,128)S(1)}, f32[4,8,2432]{2,1,0:T(8,128)S(1)}, u32[]{:S(2)}, u32[]{:S(2)}) %collective-permute-start.31) | collective-permute-done | bytes 311328 | tf_op jit(solution)/shard_map/ppermute | solution.py:36
  204.6 3.0 %collective-permute-start.33 = (f32[1,8,2432]{2,1,0:T(8,128)S(1)}, f32[1,8,2432]{2,1,0:T(8,128)S(1)}, u32[]{:S(2)}, u32[]{:S(2)}) collective-permute-start(f32[1,8,2432]{2,1,0:T(8,128)S(1)} %get-tuple-element.89), channel_id=1, source_target_pairs={{0,16},{1,17},{2,18},{3,19},{4,20},{5,21},{6,22},{7,23},{8,24},{9,... | collective-permute-start | bytes 233480 | tf_op jit(solution)/shard_map/ppermute | solution.py:36
  210.4 2.6 %collective-permute-done.33 = f32[1,8,2432]{2,1,0:T(8,128)S(1)} collective-permute-done((f32[1,8,2432]{2,1,0:T(8,128)S(1)}, f32[1,8,2432]{2,1,0:T(8,128)S(1)}, u32[]{:S(2)}, u32[]{:S(2)}) %collective-permute-start.33) | collective-permute-done | bytes 77856 | tf_op jit(solution)/shard_map/ppermute | solution.py:36
  216.9 3.1 %collective-permute-start.35 = (f32[1,16,896]{2,1,0:T(8,128)}, f32[1,16,896]{2,1,0:T(8,128)S(1)}, u32[]{:S(2)}, u32[]{:S(2)}) collective-permute-start(f32[1,16,896]{2,1,0:T(8,128)} %bitcast.44), channel_id=1, source_target_pairs={{0,8},{1,9},{2,10},{3,11},{4,12},{5,13},{6,14},{7,15},{8,0},{9,1},... | collective-permute-start | bytes 172040 | tf_op jit(solution)/shard_map/ppermute | solution.py:36
  227.5 5.4 %collective-permute-done.38 = f32[4,16,896]{2,1,0:T(8,128)S(1)} collective-permute-done((f32[4,16,896]{2,1,0:T(8,128)S(1)}, f32[4,16,896]{2,1,0:T(8,128)S(1)}, u32[]{:S(2)}, u32[]{:S(2)}) %collective-permute-start.38) | collective-permute-done | bytes 229408 | tf_op jit(solution)/shard_map/ppermute | solution.py:36
  236.9 2.7 %place.1 = (f32[512,768]{1,0:T(8,128)}, f32[3,512]{1,0:T(4,128)}) custom-call(s32[3]{0:T(128)} %pad_add_fusion.place, f32[16,16,896]{2,1,0:T(8,128)} %copy-done.11, f32[16,16,896]{2,1,0:T(8,128)} %copy-done.12), custom_call_target="tpu_custom_call" | custom-call | tf_op jit(solution)/shard_map/place/pallas_call | solution.py:366
  (183 shorter events, 92.9 us)
Async XLA Ops:
  22.4 11.1 %collective-permute-start.1 = (f32[4,8,2432]{2,1,0:T(8,128)S(1)}, f32[4,8,2432]{2,1,0:T(8,128)S(1)}, u32[]{:S(2)}, u32[]{:S(2)}) collective-permute-start(f32[4,8,2432]{2,1,0:T(8,128)S(1)} %get-tuple-element.84), channel_id=1, source_target_pairs={{0,2},{1,3},{2,0},{3,1},{4,6},{5,7},{6,4},{7,5},{8,10},{9,11},{10,... | collective-permute-start | bytes 933896 | tf_op jit(solution)/shard_map/ppermute | solution.py:36
  25.3 15.6 %collective-permute-start.3 = (f32[4,8,2432]{2,1,0:T(8,128)S(1)}, f32[4,8,2432]{2,1,0:T(8,128)S(1)}, u32[]{:S(2)}, u32[]{:S(2)}) collective-permute-start(f32[4,8,2432]{2,1,0:T(8,128)S(1)} %get-tuple-element.85), channel_id=1, source_target_pairs={{0,6},{1,7},{2,4},{3,5},{4,2},{5,3},{6,0},{7,1},{8,14},{9,15},{10,... | collective-permute-start | bytes 933896 | tf_op jit(solution)/shard_map/ppermute | solution.py:36
  26.8 15.6 %collective-permute-start.2 = (f32[4,8,2432]{2,1,0:T(8,128)S(1)}, f32[4,8,2432]{2,1,0:T(8,128)}, u32[]{:S(2)}, u32[]{:S(2)}) collective-permute-start(f32[4,8,2432]{2,1,0:T(8,128)S(1)} %get-tuple-element.86), channel_id=1, source_target_pairs={{0,4},{1,5},{2,6},{3,7},{4,0},{5,1},{6,2},{7,3},{8,12},{9,13},{10,... | collective-permute-start | bytes 933896 | tf_op jit(solution)/shard_map/ppermute | solution.py:36
  62.3 12.8 %collective-permute-start.12 = (f32[4,8,2432]{2,1,0:T(8,128)S(1)}, f32[4,8,2432]{2,1,0:T(8,128)S(1)}, u32[]{:S(2)}, u32[]{:S(2)}) collective-permute-start(f32[4,8,2432]{2,1,0:T(8,128)S(1)} %pad_maximum_fusion), channel_id=1, source_target_pairs={{0,6},{1,7},{2,4},{3,5},{4,2},{5,3},{6,0},{7,1},{8,14},{9,15},{10,... | collective-permute-start | bytes 933896 | tf_op jit(solution)/shard_map/ppermute | solution.py:36
  63.8 11.3 %collective-permute-start.11 = (f32[4,8,2432]{2,1,0:T(8,128)S(1)}, f32[4,8,2432]{2,1,0:T(8,128)S(1)}, u32[]{:S(2)}, u32[]{:S(2)}) collective-permute-start(f32[4,8,2432]{2,1,0:T(8,128)S(1)} %pad_maximum_fusion), channel_id=1, source_target_pairs={{0,4},{1,5},{2,6},{3,7},{4,0},{5,1},{6,2},{7,3},{8,12},{9,13},{10,... | collective-permute-start | bytes 933896 | tf_op jit(solution)/shard_map/ppermute | solution.py:36
  65.3 9.0 %collective-permute-start.10 = (f32[4,8,2432]{2,1,0:T(8,128)S(1)}, f32[4,8,2432]{2,1,0:T(8,128)S(1)}, u32[]{:S(2)}, u32[]{:S(2)}) collective-permute-start(f32[4,8,2432]{2,1,0:T(8,128)S(1)} %pad_maximum_fusion), channel_id=1, source_target_pairs={{0,2},{1,3},{2,0},{3,1},{4,6},{5,7},{6,4},{7,5},{8,10},{9,11},{10,... | collective-permute-start | bytes 933896 | tf_op jit(solution)/shard_map/ppermute | solution.py:36
  106.5 22.1 %collective-permute-start.14 = (f32[16,8,2432]{2,1,0:T(8,128)}, f32[16,8,2432]{2,1,0:T(8,128)S(1)}, u32[]{:S(2)}, u32[]{:S(2)}) collective-permute-start(f32[16,8,2432]{2,1,0:T(8,128)} %get-tuple-element.44), channel_id=1, source_target_pairs={{0,1},{1,0},{2,3},{3,2},{4,5},{5,4},{6,7},{7,6},{8,9},{9,8},{10,11... | collective-permute-start | bytes 3735560 | tf_op jit(solution)/shard_map/ppermute | solution.py:36
  125.8 20.3 %all-to-all-start.1 = ((f32[32,8,256]{2,1,0:T(8,128)}), f32[32,8,256]{2,1,0:T(8,128)S(1)}, u32[]{:S(2)}, u32[]{:S(2)}) async-start(f32[32,8,256]{2,1,0:T(8,128)} %get-tuple-element.53), calls=%async_computation.1 | async-start | bytes 524288 | tf_op jit(solution)/shard_map/all_to_all | solution.py:61
  131.9 30.3 %collective-permute-start.15 = (f32[4,8,2432]{2,1,0:T(8,128)}, f32[4,8,2432]{2,1,0:T(8,128)}, u32[]{:S(2)}, u32[]{:S(2)}) collective-permute-start(f32[4,8,2432]{2,1,0:T(8,128)} %get-tuple-element.81), channel_id=1, source_target_pairs={{0,2},{1,3},{2,0},{3,1},{4,6},{5,7},{6,4},{7,5},{8,10},{9,11},{10,... | collective-permute-start | bytes 933896 | tf_op jit(solution)/shard_map/ppermute | solution.py:36
  133.3 28.9 %collective-permute-start.17 = (f32[4,8,2432]{2,1,0:T(8,128)S(1)}, f32[4,8,2432]{2,1,0:T(8,128)}, u32[]{:S(2)}, u32[]{:S(2)}) collective-permute-start(f32[4,8,2432]{2,1,0:T(8,128)S(1)} %get-tuple-element.82), channel_id=1, source_target_pairs={{0,6},{1,7},{2,4},{3,5},{4,2},{5,3},{6,0},{7,1},{8,14},{9,15},{10,... | collective-permute-start | bytes 933896 | tf_op jit(solution)/shard_map/ppermute | solution.py:36
  134.8 27.4 %collective-permute-start.16 = (f32[4,8,2432]{2,1,0:T(8,128)S(1)}, f32[4,8,2432]{2,1,0:T(8,128)}, u32[]{:S(2)}, u32[]{:S(2)}) collective-permute-start(f32[4,8,2432]{2,1,0:T(8,128)S(1)} %get-tuple-element.83), channel_id=1, source_target_pairs={{0,4},{1,5},{2,6},{3,7},{4,0},{5,1},{6,2},{7,3},{8,12},{9,13},{10,... | collective-permute-start | bytes 933896 | tf_op jit(solution)/shard_map/ppermute | solution.py:36
  146.1 21.3 %collective-permute-start.21 = (f32[16,8,2432]{2,1,0:T(8,128)}, f32[16,8,2432]{2,1,0:T(8,128)S(1)}, u32[]{:S(2)}, u32[]{:S(2)}) collective-permute-start(f32[16,8,2432]{2,1,0:T(8,128)} %get-tuple-element.52), channel_id=1, source_target_pairs={{0,1},{1,0},{2,3},{3,2},{4,5},{5,4},{6,7},{7,6},{8,9},{9,8},{10,11... | collective-permute-start | bytes 3735560 | tf_op jit(solution)/shard_map/ppermute | solution.py:36
  161.7 25.3 %collective-permute-start.28 = (f32[16,8,2432]{2,1,0:T(8,128)}, f32[16,8,2432]{2,1,0:T(8,128)S(1)}, u32[]{:S(2)}, u32[]{:S(2)}) collective-permute-start(f32[16,8,2432]{2,1,0:T(8,128)} %get-tuple-element.59), channel_id=1, source_target_pairs={{0,1},{1,0},{2,3},{3,2},{4,5},{5,4},{6,7},{7,6},{8,9},{9,8},{10,11... | collective-permute-start | bytes 3735560 | tf_op jit(solution)/shard_map/ppermute | solution.py:36
  167.7 10.3 %collective-permute-start.22 = (f32[4,8,2432]{2,1,0:T(8,128)S(1)}, f32[4,8,2432]{2,1,0:T(8,128)S(1)}, u32[]{:S(2)}, u32[]{:S(2)}) collective-permute-start(f32[4,8,2432]{2,1,0:T(8,128)S(1)} %get-tuple-element.78), channel_id=1, source_target_pairs={{0,2},{1,3},{2,0},{3,1},{4,6},{5,7},{6,4},{7,5},{8,10},{9,11},{10,... | collective-permute-start | bytes 933896 | tf_op jit(solution)/shard_map/ppermute | solution.py:36
  169.2 15.0 %collective-permute-start.24 = (f32[4,8,2432]{2,1,0:T(8,128)S(1)}, f32[4,8,2432]{2,1,0:T(8,128)S(1)}, u32[]{:S(2)}, u32[]{:S(2)}) collective-permute-start(f32[4,8,2432]{2,1,0:T(8,128)S(1)} %get-tuple-element.79), channel_id=1, source_target_pairs={{0,6},{1,7},{2,4},{3,5},{4,2},{5,3},{6,0},{7,1},{8,14},{9,15},{10,... | collective-permute-start | bytes 933896 | tf_op jit(solution)/shard_map/ppermute | solution.py:36
  172.1 14.8 %collective-permute-start.23 = (f32[4,8,2432]{2,1,0:T(8,128)S(1)}, f32[4,8,2432]{2,1,0:T(8,128)S(1)}, u32[]{:S(2)}, u32[]{:S(2)}) collective-permute-start(f32[4,8,2432]{2,1,0:T(8,128)S(1)} %get-tuple-element.80), channel_id=1, source_target_pairs={{0,4},{1,5},{2,6},{3,7},{4,0},{5,1},{6,2},{7,3},{8,12},{9,13},{10,... | collective-permute-start | bytes 933896 | tf_op jit(solution)/shard_map/ppermute | solution.py:36
  187.2 10.3 %collective-permute-start.29 = (f32[4,8,2432]{2,1,0:T(8,128)S(1)}, f32[4,8,2432]{2,1,0:T(8,128)S(1)}, u32[]{:S(2)}, u32[]{:S(2)}) collective-permute-start(f32[4,8,2432]{2,1,0:T(8,128)S(1)} %get-tuple-element.75), channel_id=1, source_target_pairs={{0,2},{1,3},{2,0},{3,1},{4,6},{5,7},{6,4},{7,5},{8,10},{9,11},{10,... | collective-permute-start | bytes 933896 | tf_op jit(solution)/shard_map/ppermute | solution.py:36
  188.8 13.8 %collective-permute-start.31 = (f32[4,8,2432]{2,1,0:T(8,128)S(1)}, f32[4,8,2432]{2,1,0:T(8,128)S(1)}, u32[]{:S(2)}, u32[]{:S(2)}) collective-permute-start(f32[4,8,2432]{2,1,0:T(8,128)S(1)} %get-tuple-element.76), channel_id=1, source_target_pairs={{0,6},{1,7},{2,4},{3,5},{4,2},{5,3},{6,0},{7,1},{8,14},{9,15},{10,... | collective-permute-start | bytes 933896 | tf_op jit(solution)/shard_map/ppermute | solution.py:36
  190.2 13.7 %collective-permute-start.30 = (f32[4,8,2432]{2,1,0:T(8,128)S(1)}, f32[4,8,2432]{2,1,0:T(8,128)S(1)}, u32[]{:S(2)}, u32[]{:S(2)}) collective-permute-start(f32[4,8,2432]{2,1,0:T(8,128)S(1)} %get-tuple-element.77), channel_id=1, source_target_pairs={{0,4},{1,5},{2,6},{3,7},{4,0},{5,1},{6,2},{7,3},{8,12},{9,13},{10,... | collective-permute-start | bytes 933896 | tf_op jit(solution)/shard_map/ppermute | solution.py:36
  190.8 13.8 %collective-permute-start.25 = (f32[1,8,2432]{2,1,0:T(8,128)S(1)}, f32[1,8,2432]{2,1,0:T(8,128)S(1)}, u32[]{:S(2)}, u32[]{:S(2)}) collective-permute-start(f32[1,8,2432]{2,1,0:T(8,128)S(1)} %get-tuple-element.90), channel_id=1, source_target_pairs={{0,8},{1,9},{2,10},{3,11},{4,12},{5,13},{6,14},{7,15},{8,0},{9,1},... | collective-permute-start | bytes 233480 | tf_op jit(solution)/shard_map/ppermute | solution.py:36
  191.3 16.2 %collective-permute-start.27 = (f32[1,8,2432]{2,1,0:T(8,128)S(1)}, f32[1,8,2432]{2,1,0:T(8,128)S(1)}, u32[]{:S(2)}, u32[]{:S(2)}) collective-permute-start(f32[1,8,2432]{2,1,0:T(8,128)S(1)} %get-tuple-element.91), channel_id=1, source_target_pairs={{0,24},{1,25},{2,26},{3,27},{4,28},{5,29},{6,30},{7,31},{8,16},{9,... | collective-permute-start | bytes 233480 | tf_op jit(solution)/shard_map/ppermute | solution.py:36
  197.5 10.1 %collective-permute-start.26 = (f32[1,8,2432]{2,1,0:T(8,128)S(1)}, f32[1,8,2432]{2,1,0:T(8,128)S(1)}, u32[]{:S(2)}, u32[]{:S(2)}) collective-permute-start(f32[1,8,2432]{2,1,0:T(8,128)S(1)} %get-tuple-element.92), channel_id=1, source_target_pairs={{0,16},{1,17},{2,18},{3,19},{4,20},{5,21},{6,22},{7,23},{8,24},{9,... | collective-permute-start | bytes 233480 | tf_op jit(solution)/shard_map/ppermute | solution.py:36
  204.6 8.4 %collective-permute-start.33 = (f32[1,8,2432]{2,1,0:T(8,128)S(1)}, f32[1,8,2432]{2,1,0:T(8,128)S(1)}, u32[]{:S(2)}, u32[]{:S(2)}) collective-permute-start(f32[1,8,2432]{2,1,0:T(8,128)S(1)} %get-tuple-element.89), channel_id=1, source_target_pairs={{0,16},{1,17},{2,18},{3,19},{4,20},{5,21},{6,22},{7,23},{8,24},{9,... | collective-permute-start | bytes 233480 | tf_op jit(solution)/shard_map/ppermute | solution.py:36
  223.9 9.5 %collective-permute-start.40 = (f32[4,16,896]{2,1,0:T(8,128)S(1)}, f32[4,16,896]{2,1,0:T(8,128)S(1)}, u32[]{:S(2)}, u32[]{:S(2)}) collective-permute-start(f32[4,16,896]{2,1,0:T(8,128)S(1)} %pad_maximum_fusion.1), channel_id=1, source_target_pairs={{0,6},{1,7},{2,4},{3,5},{4,2},{5,3},{6,0},{7,1},{8,14},{9,15},{10,... | collective-permute-start | bytes 688136 | tf_op jit(solution)/shard_map/ppermute | solution.py:36
  (40 other events, 414.2 us)

commit v2 on v1

v2 whole, which is shorter than its diff:
```python
import functools

import jax
import jax.numpy as jnp
from jax import lax
from jax.experimental import pallas as pl
from jax.experimental.pallas import tpu as pltpu
from jax.sharding import PartitionSpec as P

AXES = ("rows", "hosts")
LANES = 128
F32 = jnp.float32
BF16 = jnp.bfloat16


class Comm:
    def __init__(self, devices, most_blocks):
        self.n = devices
        self.me = lax.axis_index(AXES)
        bits = devices.bit_length() - 1
        assert 1 << bits == devices
        radices = [2] * (bits % 2) + [4] * (bits // 2)
        self.stages, self.extra = [], []
        self.blocks, stride, self.block = 1, 1, 0
        for radix in radices:
            if self.blocks * radix <= most_blocks:
                self.stages.append((radix, stride))
                self.block = self.block * radix + (self.me // stride) % radix
                self.blocks *= radix
            else:
                self.extra.append((radix, stride))
            stride *= radix
        self.lead = self.stages[0][0]

    def send(self, x, mask):
        return lax.ppermute(x, AXES, [(i, i ^ mask) for i in range(self.n)])

    def reduce_scatter(self, pieces):
        for step, (radix, stride) in enumerate(self.stages):
            if step:
                x = x.reshape((radix, x.shape[0] // radix) + x.shape[1:])
                pieces = [x[j] for j in range(radix)]
            got = [self.send(pieces[j], j * stride) for j in range(1, radix)]
            x = functools.reduce(jnp.add, got, pieces[0])
        x = x[0]
        for radix, stride in self.extra:
            while radix > 1:
                x = x + self.send(x, stride)
                stride, radix = stride * 2, radix // 2
        return x

    def all_gather(self, x):
        x = x[None]
        for radix, stride in self.stages[::-1]:
            pieces = [x] + [self.send(x, j * stride) for j in range(1, radix)]
            if (radix, stride) != self.stages[0]:
                x = jnp.concatenate(pieces)
        return pieces

    def share(self, x):
        return lax.all_to_all(x, AXES, 0, 0, tiled=True)


def dot(a, b):
    return lax.dot_general(a, b, (((1,), (0,)), ((), ())), preferred_element_type=F32)


def dot_t(a, b):
    return lax.dot_general(a, b, (((1,), (1,)), ((), ())), preferred_element_type=F32)


def split2(x):
    high = x.astype(BF16)
    return high, (x - high.astype(F32)).astype(BF16)


def iota(shape, axis):
    return lax.broadcasted_iota(jnp.int32, shape, axis)


def lane_sum(x):
    return jnp.sum(x, axis=1, keepdims=True)


def pack(columns):
    rows = columns[0].shape[0]
    lane = iota((rows, LANES), 1)
    out = jnp.zeros((rows, LANES), F32)
    for q, c in enumerate(columns):
        out = jnp.where(lane == q, c, out)
    return out


def to_blocks(scratch, outs, block, own, per):
    for j, out in enumerate(outs):
        for t in range(per):
            at = (block ^ (j * per + t)) * own
            out[t] = scratch[pl.ds(pl.multiple_of(at, 8), own), :]


def lanes(ref, l, width):
    return ref[:, l * width : (l + 1) * width]


def columns_of(rows):
    fill = jnp.zeros((LANES - rows.shape[0], rows.shape[1]), F32)
    return jnp.transpose(jnp.concatenate([rows, fill], axis=0))


def seed_columns(seeds, first_row):
    levels = seeds.shape[0]
    rows = [seeds[l].astype(F32) - first_row for l in range(levels)]
    return rows, columns_of(jnp.concatenate(rows, axis=0))


def halves_hot(found, row, l):
    hot0 = jnp.where(found[:, 2 * l : 2 * l + 1] == row, 0.5, 0.0)
    hot1 = jnp.where(found[:, 2 * l + 1 : 2 * l + 2] == row, 0.5, 0.0)
    return hot0, hot1


def pick_kernel(place, seeds, emb, *refs, levels, lead, per, own):
    outs = refs[:lead]
    high, low, squares, scratch = refs[lead:]
    rows, width = emb.shape
    splits = seeds.shape[2]
    e = emb[...]
    a, b = split2(e)
    high[...] = a
    low[...] = b
    column = lane_sum(e * e)
    sq = jnp.transpose(jnp.broadcast_to(column, (rows, LANES)))[0:1, :]
    squares[...] = sq
    _, found = seed_columns(seeds, place[1].astype(F32))
    row = iota((splits, rows), 1).astype(F32)
    bs = []
    for l in range(levels):
        hot0, hot1 = halves_hot(found, row, l)
        hot = hot0 - hot1
        d = hot.astype(BF16)
        scratch[:, l * width : (l + 1) * width] = dot(d, a) + dot(d, b)
        bs.append(0.5 * lane_sum(hot * sq))
    scratch[:, levels * width :] = pack(bs)
    to_blocks(scratch, outs, place[0], own, per)


def tables_kernel(place, seeds, order, root, high, low, cols, *refs, levels):
    means, deltas, roots = refs[:levels], refs[levels : 2 * levels], refs[2 * levels :]
    rows, width = high.shape
    splits = seeds.shape[2]
    seed_rows, found = seed_columns(seeds, place[1].astype(F32))
    order_rows = order[...][:, :splits].astype(F32)
    order_cols = columns_of(order_rows)
    row = iota((splits, rows), 1).astype(F32)
    lane = iota((splits, splits), 1).astype(F32)
    cluster = iota((splits, root.shape[0]), 1).astype(F32)
    a, b = high[...], low[...]
    ra, rb = split2(root[...])
    chain, root_at = [], []
    for l in range(levels):
        node = order_cols[:, l : l + 1]
        entry = []
        for k in range(l - 1, -1, -1):
            half = jnp.floor(node * 0.5)
            odd = node - 2.0 * half
            value = jnp.where(odd > 0, seed_rows[k][1:2, :], seed_rows[k][0:1, :])
            hit = lane == half
            entry.append([half, odd, lane_sum(jnp.where(hit, value, 0.0))])
            node = lane_sum(jnp.where(hit, order_rows[k : k + 1, :], 0.0))
        for e in entry[::-1]:
            chain += e
        root_at.append(node)
        hot = jnp.where(cluster == node, 1.0, 0.0).astype(BF16)
        roots[l][...] = dot(hot, ra) + dot(hot, rb)
        hot0, hot1 = halves_hot(found, row, l)
        d, m = (hot0 - hot1).astype(BF16), (hot0 + hot1).astype(BF16)
        means[l][...] = dot(m, a) + dot(m, b)
        deltas[l][...] = dot(d, a) + dot(d, b)
    cols[...] = pack([order_cols[:, l : l + 1] for l in range(levels)] + root_at + chain)


def level_step(l, levels, offset, proj, ahead, cols, member, sq, rows_in, lookups, scale):
    splits, rows = proj.shape
    chosen = cols[:, l : l + 1] == member[l : l + 1, :].astype(F32)
    part = jnp.where(chosen, proj - offset, 0.0)
    gap = 2.0 * jnp.sum(part, axis=0, keepdims=True)
    inside = jnp.sum(jnp.where(chosen, 1.0, 0.0), axis=0, keepdims=True)
    first = jax.nn.sigmoid(gap * scale)
    number = iota((splits, rows), 0).astype(F32)
    index = jnp.sum(jnp.where(chosen, number + 1.0, 0.0), axis=0, keepdims=True) - 1.0
    w0 = jnp.where(chosen, first, 0.0)
    w1 = jnp.where(chosen, 1.0 - first, 0.0)
    columns = [lane_sum(w0), lane_sum(w1), lane_sum(w0 * sq), lane_sum(w1 * sq)]
    rows_out = rows_in + [(index, first)]
    if l + 1 < levels:
        row = iota((splits, rows), 1).astype(F32)
        coef = jnp.ones((splits, 1), F32)
        total = jnp.zeros((splits, 1), F32)
        for k in range(l, -1, -1):
            half, odd, seed = ancestor(cols, levels, l + 1, k)
            if k < l:
                coef = coef * lookups[k](half, odd)
            at, f = rows_out[k]
            w = jnp.where(at == half, jnp.where(odd > 0, 1.0 - f, f), 0.0)
            w = w + jnp.where(row == seed, 0.5, 0.0)
            total = total + coef * lane_sum(w * ahead)
            coef = 0.5 * coef
        columns += [total, coef]
    return first * inside, rows_out, columns


def ancestor(cols, levels, l, k):
    at = 2 * levels + 3 * (l * (l - 1) // 2 + k)
    return cols[:, at : at + 1], cols[:, at + 1 : at + 2], cols[:, at + 2 : at + 3]


def emit(columns, small, shared):
    packed = pack(columns)
    small[...] = packed
    if shared is not None:
        across = jnp.transpose(packed)[:8, :]
        for i in range(shared.shape[0]):
            shared[i] = across


def delta_of(pieces, block, own, per, lo, hi, scratch):
    for j, piece in enumerate(pieces):
        for t in range(per):
            at = (block ^ (j * per + t)) * own
            scratch[pl.ds(pl.multiple_of(at, 8), own), :] = piece[t, :, lo:hi]


def project(da, db, a, b):
    return dot_t(da, a) + (dot_t(da, b) + dot_t(db, a))


def project_kernel(place, *refs, levels, lead, per, own, scale):
    pieces = refs[:lead]
    high, low, squares, root0, root1, cols, member = refs[lead : lead + 7]
    proj, stat, small, shared, state, out, scratch, extra = refs[lead + 7 :]
    width = high.shape[1]
    delta_of(pieces, place[0], own, per, levels * width, levels * width + LANES, extra)
    stats = [extra[:, l : l + 1] for l in range(levels)]
    a, b = high[...], low[...]
    made = []
    for l, root in enumerate((root0, root1)):
        delta_of(pieces, place[0], own, per, l * width, (l + 1) * width, scratch)
        d = scratch[...]
        stats.append(lane_sum(d * root[...]))
        made.append(project(*split2(d), a, b))
    proj[...] = made[1]
    stat[...] = pack(stats)
    sq = squares[...]
    offset = 0.5 * (stats[levels] + stats[0])
    weight, kept, columns = level_step(
        0, levels, offset, made[0], made[1], cols, member, sq, [], [], scale
    )
    out[...] = weight
    state[...] = jnp.zeros(state.shape, F32)
    state[0:1, :] = sq
    state[1:2, :] = kept[0][0]
    state[2:3, :] = kept[0][1]
    emit(columns, small, shared)


def ahead_kernel(place, *refs, l, levels, lead, per, own):
    pieces = refs[:lead]
    high, low, root, proj, stat, scratch = refs[lead:]
    width = high.shape[1]
    delta_of(pieces, place[0], own, per, l * width, (l + 1) * width, scratch)
    d = scratch[...]
    stat[...] = jnp.broadcast_to(lane_sum(d * root[...]), stat.shape)
    proj[...] = project(*split2(d), high[...], low[...])


def level_kernel(*refs, l, levels, n, scale):
    refs = list(refs)
    got, proj = refs.pop(0), refs.pop(0)
    ahead = refs.pop(0) if l + 1 < levels else None
    stat, root_stat, before, state, cols, member = (refs.pop(0) for _ in range(6))
    counts = refs.pop(0) if l > 1 else None
    small, state_out, counts_out, out = (refs.pop(0) for _ in range(4))
    shared = refs.pop(0) if l + 1 < levels else None
    splits = proj.shape[0]
    total = got[0]
    for i in range(1, n):
        total = total + got[i]
    down = columns_of(total)
    counts_out[...] = jnp.zeros(counts_out.shape, F32) if counts is None else counts[...]
    counts_out[2 * (l - 1) : 2 * l, :] = 1.0 / (total[0:2, :] + 1.0)
    lane = iota((splits, splits), 1).astype(F32)

    def lookup(k):
        def run(half, odd):
            value = jnp.where(
                odd > 0, counts_out[2 * k + 1 : 2 * k + 2, :], counts_out[2 * k : 2 * k + 1, :]
            )
            return lane_sum(jnp.where(lane == half, value, 0.0))

        return run

    lookups = [lookup(k) for k in range(l)]
    half, odd, _ = ancestor(cols, levels, l, l - 1)
    inverse = lookups[l - 1](half, odd)
    at = levels + 1 if l == 1 else 0
    root = root_stat[:, at : at + 1]
    dots = (down[:, 4:5] + before[:, 5:6] * root) * inverse
    offset = 0.5 * (dots + stat[:, l : l + 1])
    kept = [(state[1 + 2 * k : 2 + 2 * k, :], state[2 + 2 * k : 3 + 2 * k, :]) for k in range(l)]
    weight, kept, columns = level_step(
        l,
        levels,
        offset,
        proj[...],
        None if ahead is None else ahead[...],
        cols,
        member,
        state[0:1, :],
        kept,
        lookups,
        scale,
    )
    out[...] = weight
    state_out[...] = state[...]
    state_out[1 + 2 * l : 2 + 2 * l, :] = kept[l][0]
    state_out[2 + 2 * l : 3 + 2 * l, :] = kept[l][1]
    columns = columns + [jnp.zeros((splits, 1), F32)] * (6 - len(columns)) + [inverse]
    emit(columns, small, shared)


def sums_kernel(place, order, *refs, l, levels, lead, per, own):
    refs = list(refs)
    high, low, state, small = (refs.pop(0) for _ in range(4))
    more = l + 1 < levels
    if more:
        mean, delta, start = (refs.pop(0) for _ in range(3))
    later = [refs.pop(0) for _ in range(levels - 2)] if l == 0 else []
    outs = [refs.pop(0) for _ in range(lead)]
    carry_out = refs.pop(0) if l == 0 else None
    scratch = refs.pop(0)
    tables = refs.pop(0) if more else None
    rows, width = high.shape
    splits = small.shape[0]
    number = iota((splits, rows), 0).astype(F32)
    index = state[1 + 2 * l : 2 + 2 * l, :]
    first = state[2 + 2 * l : 3 + 2 * l, :]
    chosen = number == index
    a, b = high[...], low[...]
    for j, f in enumerate((first, 1.0 - first)):
        wa, wb = split2(jnp.where(chosen, f, 0.0))
        scratch[:, j * width : (j + 1) * width] = dot(wa, a) + (dot(wa, b) + dot(wb, a))
    at = 2
    if more:
        m = mean[...]
        if l:
            mid = 0.5 * (start[...] * small[:, 6:7] + m)
            if l == 1:
                scratch[:, at * width : (at + 1) * width] = mid
                at += 1
        else:
            mid = 0.5 * (start[...] * jnp.where(place[2] == 0, 1.0, 0.0) + m)
            scratch[:, at * width : (at + 1) * width] = m
            at += 1
        half = 0.5 * delta[...]
        tables[0] = lanes(scratch, 0, width) + (mid + half)
        tables[1] = lanes(scratch, 1, width) + (mid - half)
        first_lane = at * width

        def move(s, carry):
            node = order[l + 1, s]
            value = tables[lax.rem(node, 2), pl.ds(lax.div(node, 2), 1), :]
            if l:
                scratch[pl.ds(s, 1), first_lane : first_lane + width] = value
            else:
                carry_out[pl.ds(s, 1), :] = value
            return carry

        lax.fori_loop(0, splits, move, 0, unroll=8)
        if l:
            at += 1
    for ref in later:
        scratch[:, at * width : (at + 1) * width] = ref[...]
        at += 1
    scratch[:, at * width :] = small[...]
    to_blocks(scratch, outs, place[0], own, per)


def finish_kernel(place, *refs, levels):
    sums = refs[:levels]
    smalls = refs[levels : 2 * levels - 2]
    root, delta, out = refs[2 * levels - 2 :]
    own = out.shape[0] // 2
    width = out.shape[1] - LANES
    here = pl.ds(pl.multiple_of(place[0] * own, 8), own)
    spread = []
    for l in range(levels):
        if l == 0:
            mid = 0.5 * (lanes(sums[0], 2, width) + root[here, :])
        elif l == 1:
            mid = lanes(sums[1], 2, width)
        else:
            grown = lanes(sums[l - 1], 3 if l == 2 else 2, width)
            inverse = smalls[l - 2][here, 6:7]
            mid = 0.5 * (grown * inverse + lanes(sums[0], l + 1, width))
        half = 0.5 * lanes(delta, l, width)
        last = sums[l].shape[1] - LANES
        for j in range(2):
            s = lanes(sums[l], j, width)
            count = sums[l][:, last + j : last + j + 1]
            energy = sums[l][:, last + 2 + j : last + 3 + j]
            centre = (s + (mid + half if j == 0 else mid - half)) / (count + 1.0)
            error = (
                energy - 2.0 * lane_sum(centre * s) + count * lane_sum(centre * centre)
            )
            spread.append(error / ((count + 1.0) * width))
            if l + 1 == levels:
                for i in range(own):
                    out[2 * i + j : 2 * i + j + 1, :width] = centre[i : i + 1, :]
    out[:own, width:] = pack(spread)
    out[own:, width:] = jnp.zeros((own, LANES), F32)


def place_kernel(place, *refs, levels, lead, per, own):
    pieces = refs[:lead]
    centre, spread, scratch = refs[lead:]
    splits, width = scratch.shape[0], centre.shape[1]
    for j, piece in enumerate(pieces):
        for t in range(per):
            at = (place[0] ^ (j * per + t)) * own
            centre[pl.ds(pl.multiple_of(2 * at, 8), 2 * own), :] = piece[t, :, :width]
            scratch[pl.ds(pl.multiple_of(at, 8), own), :] = piece[t, :own, width:]
    across = jnp.transpose(scratch[...])[:8, :]
    a = across.astype(BF16)
    rest = across - a.astype(F32)
    b = rest.astype(BF16)
    c = (rest - b.astype(F32)).astype(BF16)
    total = jnp.zeros((8, 2 * splits), F32)
    outs = []
    for j in range(2):
        hot = jnp.where(
            iota((splits, 2 * splits), 1) == 2 * iota((splits, 2 * splits), 0) + j, 1.0, 0.0
        ).astype(BF16)
        outs.append(dot(a, hot) + (dot(b, hot) + dot(c, hot)))
    for l in range(levels):
        spread[l : l + 1, :] = outs[0][2 * l : 2 * l + 1, :] + outs[1][2 * l + 1 : 2 * l + 2, :]


def on_device(embeddings, root_centroids, member_ids, split_order, seed_rows):
    rows, width = embeddings.shape
    levels, splits = seed_rows.shape[:2]
    assert levels == 3
    comm = Comm(lax.axis_size(AXES), splits // 8)
    n, lead = comm.n, comm.lead
    own = splits // comm.blocks
    per = comm.blocks // lead
    scale = 0.5 / (float(width) ** 0.5)
    place = jnp.stack([comm.block, comm.me * rows, comm.me]).astype(jnp.int32)
    smem = pl.BlockSpec(memory_space=pltpu.SMEM)
    vmem = pl.BlockSpec(memory_space=pltpu.VMEM)
    geometry = dict(levels=levels, lead=lead, per=per, own=own)
    table = (splits, width)
    narrow = (splits, LANES)

    def struct(shape, dtype=F32):
        return jax.ShapeDtypeStruct(shape, dtype)

    def pieces_of(parts):
        return [struct((per, own, parts * width + LANES))] * lead

    def call(kernel, name, outs, scalars, args, scratch=(), limit=30):
        run = pl.pallas_call(
            kernel,
            name=name,
            out_shape=outs,
            in_specs=[smem] * len(scalars) + [vmem] * len(args),
            out_specs=[vmem] * len(outs),
            scratch_shapes=[pltpu.VMEM(s, F32) for s in scratch],
            compiler_params=pltpu.CompilerParams(vmem_limit_bytes=limit * 1024 * 1024),
        )
        return list(run(*scalars, *args))

    seeds = seed_rows.transpose(0, 2, 1)
    *sent, high, low, squares = call(
        functools.partial(pick_kernel, **geometry),
        "pick",
        pieces_of(levels) + [struct((rows, width), BF16)] * 2 + [struct((1, rows))],
        [place],
        [seeds, embeddings],
        [(splits, levels * width + LANES)],
    )
    cols, *rest = call(
        functools.partial(tables_kernel, levels=levels),
        "tables",
        [struct(narrow)] + [struct(table)] * (3 * levels),
        [place],
        [seeds, split_order, root_centroids, high, low],
    )
    means, deltas, roots = rest[:levels], rest[levels : 2 * levels], rest[2 * levels :]
    delta_own = comm.reduce_scatter(sent)
    pieces = comm.all_gather(delta_own)
    proj, stat, small, shared, state, weight = call(
        functools.partial(project_kernel, scale=scale, **geometry),
        "project",
        [
            struct((splits, rows)),
            struct(narrow),
            struct(narrow),
            struct((n, 8, splits)),
            struct((8, rows)),
            struct((1, rows)),
        ],
        [place],
        [*pieces, high, low, squares, roots[0], roots[1], cols, member_ids],
        [table, narrow],
    )
    projs, root_stats = [None, proj], [None, stat]
    for l in range(2, levels):
        made, root_stat = call(
            functools.partial(ahead_kernel, l=l, **geometry),
            f"ahead{l}",
            [struct((splits, rows)), struct(narrow)],
            [place],
            [*pieces, high, low, roots[l]],
            [table],
        )
        projs.append(made)
        root_stats.append(root_stat)
    weights_out = [weight]
    counts, start = [], roots[0]
    sums_own, smalls = [], []
    for l in range(levels):
        more = l + 1 < levels
        if l:
            outs = [
                struct(narrow),
                struct((8, rows)),
                struct((8, splits)),
                struct((1, rows)),
            ]
            small, state, count, weight, *shared = call(
                functools.partial(level_kernel, l=l, levels=levels, n=n, scale=scale),
                f"level{l}",
                outs + [struct((n, 8, splits))] * more,
                [],
                [got, *projs[l : l + 2], stat, root_stats[l], small, state, cols, member_ids]
                + counts,
            )
            counts = [count]
            weights_out.append(weight)
            if l > 1:
                smalls.append(small)
            shared = shared[0] if more else None
        if more:
            got = comm.share(shared)
        args = [high, low, state, small]
        if more:
            args += [means[l], deltas[l], start]
        if l == 0:
            args += means[2:]
        parts = 2 + (levels - 1 if l == 0 else (l == 1) + more)
        out = call(
            functools.partial(sums_kernel, l=l, **geometry),
            f"sums{l}",
            pieces_of(parts) + [struct(table)] * (l == 0),
            [place, split_order],
            args,
            [(splits, parts * width + LANES)] + [(2, splits, width)] * more,
        )
        if l == 0:
            start = out.pop()
        sums_own.append(comm.reduce_scatter(out))
    (final,) = call(
        functools.partial(finish_kernel, levels=levels),
        "finish",
        [struct((2 * own, width + LANES))],
        [place],
        [*sums_own, *smalls, roots[0], delta_own],
    )
    pieces = comm.all_gather(final)
    centre, spread = call(
        functools.partial(place_kernel, **geometry),
        "place",
        [struct((2 * splits, width)), struct((levels, 2 * splits))],
        [place],
        pieces,
        [narrow],
    )
    return (centre, spread, jnp.concatenate(weights_out, axis=0))


def solution(mesh):
    in_specs = (P(AXES, None), P(), P(None, AXES), P(), P())
    out_specs = (P(), P(), P(None, AXES))
    return jax.shard_map(
        on_device, mesh=mesh, in_specs=in_specs, out_specs=out_specs, check_vma=False
    )
```

time: 240 us -> 230 us (0.958)
  Pallas kernels: 72.1 us -> 44.3 us
  waiting for transfers between devices: 68.5 us -> 91 us
  blocking collectives: 12.9 us -> 0 us
  starting transfers between devices: 52.4 us -> 60.8 us
  other arithmetic: 9.93 us -> 4.66 us
  local copies, waits for them, and re-layouts: 22.4 us -> 27.4 us
    pallas_call x9 -> x11, Pallas kernels: 72.1 us -> 44.3 us  [call(): return list(run(*scalars, *args))]
    unnamed x54 -> x99, local copies, waits for them, and re-layouts: 7.49 us -> 27.1 us
    ppermute x42, waiting for transfers between devices: 68.5 us -> 87.8 us  [send(): return lax.ppermute(x, AXES, [(i, i ^ mask) for i in range(self.n)])]
    all_to_all x1 -> x0, blocking collectives: 12.9 us -> none  [share(): return lax.all_to_all(x, AXES, 0, 0, tiled=True)]
    gather x6 -> x0, local copies, waits for them, and re-layouts: 11.8 us -> none  [the longest x3 6.01 us: on_device(): node = jnp.take(order[k], node // 2)]
    all_to_all x1 -> x2, starting transfers between devices: 2.8 us -> 7.19 us  [share(): return lax.all_to_all(x, AXES, 0, 0, tiled=True)]
    ppermute x42, starting transfers between devices: 49.6 us -> 53.6 us  [send(): return lax.ppermute(x, AXES, [(i, i ^ mask) for i in range(self.n)])]
    all_to_all x1 -> x2, waiting for transfers between devices: 0.01 us -> 3.21 us  [share(): return lax.all_to_all(x, AXES, 0, 0, tiled=True)]
  transfers between devices with their start and end apart: 43 -> 44, of which waited for: 26 -> 30; matrix products, arithmetic and copies ran while one was open for 9% -> 2% of each run, Pallas kernels for 13% -> 11%
where the time goes in v2:
time: 230 us; the launch traced here: 229 us
  waiting for transfers between devices  91 us (40%)
  starting transfers between devices  60.8 us (26%)
  Pallas kernels  44.3 us (19%)
  local copies, waits for them, and re-layouts  27.4 us (12%)
  other arithmetic  4.66 us (2%)
    ppermute x42, waiting for transfers between devices, send(): return lax.ppermute(x, AXES, [(i, i ^ mask) for i in range(self.n)])  87.8 us
    ppermute x42, starting transfers between devices, send(): return lax.ppermute(x, AXES, [(i, i ^ mask) for i in range(self.n)])  53.6 us
    pallas_call x11, Pallas kernels, call(): return list(run(*scalars, *args))  44.3 us
    unnamed x99, local copies, waits for them, and re-layouts  27.1 us
    all_to_all x2, starting transfers between devices, share(): return lax.all_to_all(x, AXES, 0, 0, tiled=True)  7.19 us
  transfers between devices with their start and end apart: 44, of which 30 were waited for; matrix products, arithmetic and copies ran while one was open for 2% of the time, Pallas kernels for 11%

profile of v2, /device:TPU:0, one launch (start us, length us, event | category | flops | bytes accessed | tf_op | source)
XLA Modules:
  0.0 229.5 jit_solution(14789321843254253170)
XLA Ops:
  3.3 4.1 %pick.1 = (f32[16,8,2432]{2,1,0:T(8,128)S(1)}, f32[16,8,2432]{2,1,0:T(8,128)S(1)}, bf16[1024,768]{1,0:T(8,128)(2,1)S(1)}, bf16[1024,768]{1,0:T(8,128)(2,1)S(1)}, f32[1,1024]{1,0:T(1,128)S(1)}) custom-call(s32[3]{0:T(128)S(1)} %pad_add_fusion.place, s32[3,2,256]{2,1,0:T(2,128)S(1)} %bitcast.18, f32[1024,768]{1,0:T(8,128)S(1)} %copy-done.9), custom_call_target="tpu_custom_call" | custom-call | tf_op jit(solution)/shard_map/pick/pallas_call | solution.py:480
  8.1 2.6 %collective-permute-done = f32[16,8,2432]{2,1,0:T(8,128)S(1)} collective-permute-done((f32[16,8,2432]{2,1,0:T(8,128)S(1)}, f32[16,8,2432]{2,1,0:T(8,128)S(1)}, u32[]{:S(2)}, u32[]{:S(2)}) %collective-permute-start) | collective-permute-done | bytes 1245216 | tf_op jit(solution)/shard_map/ppermute | solution.py:36
  10.8 2.9 %collective-permute-start.1 = (f32[4,8,2432]{2,1,0:T(8,128)S(1)}, f32[4,8,2432]{2,1,0:T(8,128)S(1)}, u32[]{:S(2)}, u32[]{:S(2)}) collective-permute-start(f32[4,8,2432]{2,1,0:T(8,128)S(1)} %get-tuple-element.89), channel_id=1, source_target_pairs={{0,2},{1,3},{2,0},{3,1},{4,6},{5,7},{6,4},{7,5},{8,10},{9,11},{10,... | collective-permute-start | bytes 933896 | tf_op jit(solution)/shard_map/ppermute | solution.py:36
  15.3 6.7 %collective-permute-done.1 = f32[4,8,2432]{2,1,0:T(8,128)S(1)} collective-permute-done((f32[4,8,2432]{2,1,0:T(8,128)S(1)}, f32[4,8,2432]{2,1,0:T(8,128)S(1)}, u32[]{:S(2)}, u32[]{:S(2)}) %collective-permute-start.1) | collective-permute-done | bytes 311328 | tf_op jit(solution)/shard_map/ppermute | solution.py:36
  21.9 7.4 %collective-permute-done.3 = f32[4,8,2432]{2,1,0:T(8,128)S(1)} collective-permute-done((f32[4,8,2432]{2,1,0:T(8,128)S(1)}, f32[4,8,2432]{2,1,0:T(8,128)S(1)}, u32[]{:S(2)}, u32[]{:S(2)}) %collective-permute-start.3) | collective-permute-done | bytes 311328 | tf_op jit(solution)/shard_map/ppermute | solution.py:36
  38.8 3.1 %collective-permute-done.5 = f32[1,8,2432]{2,1,0:T(8,128)S(1)} collective-permute-done((f32[1,8,2432]{2,1,0:T(8,128)S(1)}, f32[1,8,2432]{2,1,0:T(8,128)S(1)}, u32[]{:S(2)}, u32[]{:S(2)}) %collective-permute-start.5) | collective-permute-done | bytes 77856 | tf_op jit(solution)/shard_map/ppermute | solution.py:36
  43.7 2.7 %collective-permute-start.7 = (f32[1,8,2432]{2,1,0:T(8,128)S(1)}, f32[1,8,2432]{2,1,0:T(8,128)S(1)}, u32[]{:S(2)}, u32[]{:S(2)}) collective-permute-start(f32[1,8,2432]{2,1,0:T(8,128)S(1)} %get-tuple-element.82), channel_id=1, source_target_pairs={{0,8},{1,9},{2,10},{3,11},{4,12},{5,13},{6,14},{7,15},{8,0},{9,1},... | collective-permute-start | bytes 233480 | tf_op jit(solution)/shard_map/ppermute | solution.py:36
  53.5 7.7 %collective-permute-done.10 = f32[4,8,2432]{2,1,0:T(8,128)S(1)} collective-permute-done((f32[4,8,2432]{2,1,0:T(8,128)S(1)}, f32[4,8,2432]{2,1,0:T(8,128)S(1)}, u32[]{:S(2)}, u32[]{:S(2)}) %collective-permute-start.10) | collective-permute-done | bytes 311328 | tf_op jit(solution)/shard_map/ppermute | solution.py:36
  62.4 8.3 %tables.1 = (f32[256,128]{1,0:T(8,128)S(1)}, f32[256,768]{1,0:T(8,128)S(1)}, f32[256,768]{1,0:T(8,128)S(1)}, f32[256,768]{1,0:T(8,128)S(1)}, f32[256,768]{1,0:T(...) custom-call(s32[3]{0:T(128)S(1)} %pad_add_fusion.place, ...), custom_call_target="tpu_custom_call" | custom-call | tf_op jit(solution)/shard_map/tables/pallas_call | solution.py:480
  71.6 4.4 %project.1 = (f32[256,1024]{1,0:T(8,128)S(1)}, f32[256,128]{1,0:T(8,128)S(1)}, f32[256,128]{1,0:T(8,128)S(1)}, f32[32,8,256]{2,1,0:T(8,128)S(1)}, f32[8,1024]{1,0:T(8,128)S(1)}, /*index=5*/f32[1,1024]{1,0:T(1,128)S(1)}) custom-call(s32[3]{0:T(128)S(1)} %pad_add_fusion.place, f32[16,8,2432]{2,1,0:T(8,128)S(1)} %constant_dynamic-update-slice_fusion.refs_0_, ...), custom_call_target="tpu_custom_call" | custom-call | tf_op jit(solution)/shard_map/project/pallas_call | solution.py:480
  76.8 6.9 %sums0.1 = (f32[16,8,3200]{2,1,0:T(8,128)S(1)}, f32[16,8,3200]{2,1,0:T(8,128)}, f32[256,768]{1,0:T(8,128)S(1)}) custom-call(s32[3]{0:T(128)S(1)} %pad_add_fusion.place, s32[3,512]{1,0:T(4,128)S(1)} %copy-done.33, bf16[1024,768]{1,0:T(8,128)(2,1)S(1)} %get-tuple-element.42.high.refs_2_.refs_0_, bf16[1024,768]{1,0:T(8,128)(2,1)S(1)} %get-tuple-element.43.low.refs_3_.refs_1_, ...), custom_call_target="tpu_custom_call" | custom-call | tf_op jit(solution)/shard_map/sums0/pallas_call | solution.py:480
  86.2 3.7 %all-to-all-start = ((f32[32,8,256]{2,1,0:T(8,128)}), f32[32,8,256]{2,1,0:T(8,128)}, u32[]{:S(2)}, u32[]{:S(2)}) async-start(f32[32,8,256]{2,1,0:T(8,128)} %copy-done.30), calls=%async_computation | async-start | bytes 524288 | tf_op jit(solution)/shard_map/all_to_all | solution.py:61
  97.2 3.2 %all-to-all-done.refs_0_ = f32[32,8,256]{2,1,0:T(8,128)} async-done(((f32[32,8,256]{2,1,0:T(8,128)}), f32[32,8,256]{2,1,0:T(8,128)}, u32[]{:S(2)}, u32[]{:S(2)}) %all-to-all-start) | async-done | bytes 262176 | tf_op jit(solution)/shard_map/all_to_all | solution.py:61
  103.8 3.3 %level1.1 = (f32[256,128]{1,0:T(8,128)S(1)}, f32[8,1024]{1,0:T(8,128)S(1)}, f32[8,256]{1,0:T(8,128)S(1)}, f32[1,1024]{1,0:T(1,128)S(1)}, f32[32,8,256]{2,1,0:T(8,128)S(1)}) custom-call(f32[32,8,256]{2,1,0:T(8,128)} %all-to-all-done.refs_0_, f32[256,1024]{1,0:T(8,128)S(1)} %copy-done.16, f32[256,1024]{1,0:T(8,128)S(1)} %copy-done.7, ...), custom_call_target="tpu_custom_call" | custom-call | tf_op jit(solution)/shard_map/level1/pallas_call | solution.py:480
  109.7 3.5 %all-to-all-start.1 = ((f32[32,8,256]{2,1,0:T(8,128)}), f32[32,8,256]{2,1,0:T(8,128)}, u32[]{:S(2)}, u32[]{:S(2)}) async-start(f32[32,8,256]{2,1,0:T(8,128)} %copy-done.31), calls=%async_computation.1 | async-start | bytes 524288 | tf_op jit(solution)/shard_map/all_to_all | solution.py:61
  118.3 6.9 %sums1.1 = (f32[16,8,3200]{2,1,0:T(8,128)S(1)}, f32[16,8,3200]{2,1,0:T(8,128)}) custom-call(s32[3]{0:T(128)S(1)} %pad_add_fusion.place, s32[3,512]{1,0:T(4,128)S(1)} %copy-done.33, bf16[1024,768]{1,0:T(8,128)(2,1)S(1)} %get-tuple-element.42.high.refs_2_.refs_0_, bf16[1024,768]{1,0:T(8,128)(2,1)S(1)} %get-tuple-element.43.low.refs_3_.refs_1_, ...), custom_call_target="tpu_custom_call" | custom-call | tf_op jit(solution)/shard_map/sums1/pallas_call | solution.py:480
  131.8 3.5 %sums2.1 = (f32[16,8,1664]{2,1,0:T(8,128)S(1)}, f32[16,8,1664]{2,1,0:T(8,128)S(1)}) custom-call(s32[3]{0:T(128)S(1)} %pad_add_fusion.place, s32[3,512]{1,0:T(4,128)S(1)} %copy-done.33, bf16[1024,768]{1,0:T(8,128)(2,1)S(1)} %get-tuple-element.42.high.refs_2_.refs_0_, bf16[1024,768]{1,0:T(8,128)(2,1)S(1)} %get-tuple-element.43.low.refs_3_.refs_1_, ...), custom_call_target="tpu_custom_call" | custom-call | tf_op jit(solution)/shard_map/sums2/pallas_call | solution.py:480
  142.7 7.3 %collective-permute-done.15 = f32[4,8,3200]{2,1,0:T(8,128)S(1)} collective-permute-done((f32[4,8,3200]{2,1,0:T(8,128)S(1)}, f32[4,8,3200]{2,1,0:T(8,128)S(1)}, u32[]{:S(2)}, u32[]{:S(2)}) %collective-permute-start.15) | collective-permute-done | bytes 409632 | tf_op jit(solution)/shard_map/ppermute | solution.py:36
  152.2 7.3 %collective-permute-done.17 = f32[4,8,3200]{2,1,0:T(8,128)S(1)} collective-permute-done((f32[4,8,3200]{2,1,0:T(8,128)S(1)}, f32[4,8,3200]{2,1,0:T(8,128)S(1)}, u32[]{:S(2)}, u32[]{:S(2)}) %collective-permute-start.17) | collective-permute-done | bytes 409632 | tf_op jit(solution)/shard_map/ppermute | solution.py:36
  163.3 3.4 %collective-permute-start.20 = (f32[1,8,3200]{2,1,0:T(8,128)S(1)}, f32[1,8,3200]{2,1,0:T(8,128)S(1)}, u32[]{:S(2)}, u32[]{:S(2)}) collective-permute-start(f32[1,8,3200]{2,1,0:T(8,128)S(1)} %get-tuple-element.99), channel_id=1, source_target_pairs={{0,24},{1,25},{2,26},{3,27},{4,28},{5,29},{6,30},{7,31},{8,16},{9,... | collective-permute-start | bytes 307208 | tf_op jit(solution)/shard_map/ppermute | solution.py:36
  180.3 7.8 %collective-permute-done.22 = f32[4,8,3200]{2,1,0:T(8,128)S(1)} collective-permute-done((f32[4,8,3200]{2,1,0:T(8,128)S(1)}, f32[4,8,3200]{2,1,0:T(8,128)S(1)}, u32[]{:S(2)}, u32[]{:S(2)}) %collective-permute-start.22) | collective-permute-done | bytes 409632 | tf_op jit(solution)/shard_map/ppermute | solution.py:36
  188.1 2.8 %collective-permute-start.19 = (f32[1,8,3200]{2,1,0:T(8,128)S(1)}, f32[1,8,3200]{2,1,0:T(8,128)S(1)}, u32[]{:S(2)}, u32[]{:S(2)}) collective-permute-start(f32[1,8,3200]{2,1,0:T(8,128)S(1)} %get-tuple-element.100), channel_id=1, source_target_pairs={{0,16},{1,17},{2,18},{3,19},{4,20},{5,21},{6,22},{7,23},{8,24},{9,... | collective-permute-start | bytes 307208 | tf_op jit(solution)/shard_map/ppermute | solution.py:36
  202.6 4.8 %collective-permute-done.26 = f32[1,8,3200]{2,1,0:T(8,128)S(1)} collective-permute-done((f32[1,8,3200]{2,1,0:T(8,128)S(1)}, f32[1,8,3200]{2,1,0:T(8,128)S(1)}, u32[]{:S(2)}, u32[]{:S(2)}) %collective-permute-start.26) | collective-permute-done | bytes 102432 | tf_op jit(solution)/shard_map/ppermute | solution.py:36
  219.2 5.6 %collective-permute-done.38 = f32[4,16,896]{2,1,0:T(8,128)S(1)} collective-permute-done((f32[4,16,896]{2,1,0:T(8,128)S(1)}, f32[4,16,896]{2,1,0:T(8,128)S(1)}, u32[]{:S(2)}, u32[]{:S(2)}) %collective-permute-start.38) | collective-permute-done | bytes 229408 | tf_op jit(solution)/shard_map/ppermute | solution.py:36
  (200 shorter events, 108.4 us)
Async XLA Ops:
  10.8 11.1 %collective-permute-start.1 = (f32[4,8,2432]{2,1,0:T(8,128)S(1)}, f32[4,8,2432]{2,1,0:T(8,128)S(1)}, u32[]{:S(2)}, u32[]{:S(2)}) collective-permute-start(f32[4,8,2432]{2,1,0:T(8,128)S(1)} %get-tuple-element.89), channel_id=1, source_target_pairs={{0,2},{1,3},{2,0},{3,1},{4,6},{5,7},{6,4},{7,5},{8,10},{9,11},{10,... | collective-permute-start | bytes 933896 | tf_op jit(solution)/shard_map/ppermute | solution.py:36
  13.7 15.6 %collective-permute-start.3 = (f32[4,8,2432]{2,1,0:T(8,128)S(1)}, f32[4,8,2432]{2,1,0:T(8,128)S(1)}, u32[]{:S(2)}, u32[]{:S(2)}) collective-permute-start(f32[4,8,2432]{2,1,0:T(8,128)S(1)} %get-tuple-element.90), channel_id=1, source_target_pairs={{0,6},{1,7},{2,4},{3,5},{4,2},{5,3},{6,0},{7,1},{8,14},{9,15},{10,... | collective-permute-start | bytes 933896 | tf_op jit(solution)/shard_map/ppermute | solution.py:36
  15.2 15.5 %collective-permute-start.2 = (f32[4,8,2432]{2,1,0:T(8,128)S(1)}, f32[4,8,2432]{2,1,0:T(8,128)S(1)}, u32[]{:S(2)}, u32[]{:S(2)}) collective-permute-start(f32[4,8,2432]{2,1,0:T(8,128)S(1)} %get-tuple-element.91), channel_id=1, source_target_pairs={{0,4},{1,5},{2,6},{3,7},{4,0},{5,1},{6,2},{7,3},{8,12},{9,13},{10,... | collective-permute-start | bytes 933896 | tf_op jit(solution)/shard_map/ppermute | solution.py:36
  49.9 12.3 %collective-permute-start.12 = (f32[4,8,2432]{2,1,0:T(8,128)S(1)}, f32[4,8,2432]{2,1,0:T(8,128)S(1)}, u32[]{:S(2)}, u32[]{:S(2)}) collective-permute-start(f32[4,8,2432]{2,1,0:T(8,128)S(1)} %pad_maximum_fusion), channel_id=1, source_target_pairs={{0,6},{1,7},{2,4},{3,5},{4,2},{5,3},{6,0},{7,1},{8,14},{9,15},{10,... | collective-permute-start | bytes 933896 | tf_op jit(solution)/shard_map/ppermute | solution.py:36
  51.4 10.7 %collective-permute-start.11 = (f32[4,8,2432]{2,1,0:T(8,128)S(1)}, f32[4,8,2432]{2,1,0:T(8,128)S(1)}, u32[]{:S(2)}, u32[]{:S(2)}) collective-permute-start(f32[4,8,2432]{2,1,0:T(8,128)S(1)} %pad_maximum_fusion), channel_id=1, source_target_pairs={{0,4},{1,5},{2,6},{3,7},{4,0},{5,1},{6,2},{7,3},{8,12},{9,13},{10,... | collective-permute-start | bytes 933896 | tf_op jit(solution)/shard_map/ppermute | solution.py:36
  62.2 9.4 %collective-permute-start.13 = (f32[16,8,2432]{2,1,0:T(8,128)S(1)}, f32[16,8,2432]{2,1,0:T(8,128)S(1)}, u32[]{:S(2)}, u32[]{:S(2)}) collective-permute-start(f32[16,8,2432]{2,1,0:T(8,128)S(1)} %constant_dynamic-update-slice_fusion.refs_0_), channel_id=1, source_target_pairs={{0,1},{1,0},{2,3},{3,2},{4,5},{5,4},{6,7},{7,6},{8,9},{9,8},{10,11... | collective-permute-start | bytes 3735560 | tf_op jit(solution)/shard_map/ppermute | solution.py:36
  85.7 50.1 %collective-permute-start.14 = (f32[16,8,3200]{2,1,0:T(8,128)}, f32[16,8,3200]{2,1,0:T(8,128)}, u32[]{:S(2)}, u32[]{:S(2)}) collective-permute-start(f32[16,8,3200]{2,1,0:T(8,128)} %get-tuple-element.56), channel_id=1, source_target_pairs={{0,1},{1,0},{2,3},{3,2},{4,5},{5,4},{6,7},{7,6},{8,9},{9,8},{10,11... | collective-permute-start | bytes 4915208 | tf_op jit(solution)/shard_map/ppermute | solution.py:36
  86.2 14.2 %all-to-all-start = ((f32[32,8,256]{2,1,0:T(8,128)}), f32[32,8,256]{2,1,0:T(8,128)}, u32[]{:S(2)}, u32[]{:S(2)}) async-start(f32[32,8,256]{2,1,0:T(8,128)} %copy-done.30), calls=%async_computation | async-start | bytes 524288 | tf_op jit(solution)/shard_map/all_to_all | solution.py:61
  109.7 16.8 %all-to-all-start.1 = ((f32[32,8,256]{2,1,0:T(8,128)}), f32[32,8,256]{2,1,0:T(8,128)}, u32[]{:S(2)}, u32[]{:S(2)}) async-start(f32[32,8,256]{2,1,0:T(8,128)} %copy-done.31), calls=%async_computation.1 | async-start | bytes 524288 | tf_op jit(solution)/shard_map/all_to_all | solution.py:61
  126.4 47.4 %collective-permute-start.21 = (f32[16,8,3200]{2,1,0:T(8,128)}, f32[16,8,3200]{2,1,0:T(8,128)}, u32[]{:S(2)}, u32[]{:S(2)}) collective-permute-start(f32[16,8,3200]{2,1,0:T(8,128)} %get-tuple-element.68), channel_id=1, source_target_pairs={{0,1},{1,0},{2,3},{3,2},{4,5},{5,4},{6,7},{7,6},{8,9},{9,8},{10,11... | collective-permute-start | bytes 4915208 | tf_op jit(solution)/shard_map/ppermute | solution.py:36
  137.5 12.4 %collective-permute-start.15 = (f32[4,8,3200]{2,1,0:T(8,128)S(1)}, f32[4,8,3200]{2,1,0:T(8,128)S(1)}, u32[]{:S(2)}, u32[]{:S(2)}) collective-permute-start(f32[4,8,3200]{2,1,0:T(8,128)S(1)} %get-tuple-element.86), channel_id=1, source_target_pairs={{0,2},{1,3},{2,0},{3,1},{4,6},{5,7},{6,4},{7,5},{8,10},{9,11},{10,... | collective-permute-start | bytes 1228808 | tf_op jit(solution)/shard_map/ppermute | solution.py:36
  139.0 20.6 %collective-permute-start.17 = (f32[4,8,3200]{2,1,0:T(8,128)S(1)}, f32[4,8,3200]{2,1,0:T(8,128)S(1)}, u32[]{:S(2)}, u32[]{:S(2)}) collective-permute-start(f32[4,8,3200]{2,1,0:T(8,128)S(1)} %get-tuple-element.87), channel_id=1, source_target_pairs={{0,6},{1,7},{2,4},{3,5},{4,2},{5,3},{6,0},{7,1},{8,14},{9,15},{10,... | collective-permute-start | bytes 1228808 | tf_op jit(solution)/shard_map/ppermute | solution.py:36
  140.4 19.8 %collective-permute-start.16 = (f32[4,8,3200]{2,1,0:T(8,128)S(1)}, f32[4,8,3200]{2,1,0:T(8,128)S(1)}, u32[]{:S(2)}, u32[]{:S(2)}) collective-permute-start(f32[4,8,3200]{2,1,0:T(8,128)S(1)} %get-tuple-element.88), channel_id=1, source_target_pairs={{0,4},{1,5},{2,6},{3,7},{4,0},{5,1},{6,2},{7,3},{8,12},{9,13},{10,... | collective-permute-start | bytes 1228808 | tf_op jit(solution)/shard_map/ppermute | solution.py:36
  141.3 22.1 %collective-permute-start.29 = (f32[4,8,1664]{2,1,0:T(8,128)S(1)}, f32[4,8,1664]{2,1,0:T(8,128)S(1)}, u32[]{:S(2)}, u32[]{:S(2)}) collective-permute-start(f32[4,8,1664]{2,1,0:T(8,128)S(1)} %get-tuple-element.92), channel_id=1, source_target_pairs={{0,2},{1,3},{2,0},{3,1},{4,6},{5,7},{6,4},{7,5},{8,10},{9,11},{10,... | collective-permute-start | bytes 638984 | tf_op jit(solution)/shard_map/ppermute | solution.py:36
  150.0 18.0 %collective-permute-start.31 = (f32[4,8,1664]{2,1,0:T(8,128)S(1)}, f32[4,8,1664]{2,1,0:T(8,128)S(1)}, u32[]{:S(2)}, u32[]{:S(2)}) collective-permute-start(f32[4,8,1664]{2,1,0:T(8,128)S(1)} %get-tuple-element.93), channel_id=1, source_target_pairs={{0,6},{1,7},{2,4},{3,5},{4,2},{5,3},{6,0},{7,1},{8,14},{9,15},{10,... | collective-permute-start | bytes 638984 | tf_op jit(solution)/shard_map/ppermute | solution.py:36
  159.6 10.1 %collective-permute-start.30 = (f32[4,8,1664]{2,1,0:T(8,128)S(1)}, f32[4,8,1664]{2,1,0:T(8,128)S(1)}, u32[]{:S(2)}, u32[]{:S(2)}) collective-permute-start(f32[4,8,1664]{2,1,0:T(8,128)S(1)} %get-tuple-element.94), channel_id=1, source_target_pairs={{0,4},{1,5},{2,6},{3,7},{4,0},{5,1},{6,2},{7,3},{8,12},{9,13},{10,... | collective-permute-start | bytes 638984 | tf_op jit(solution)/shard_map/ppermute | solution.py:36
  160.4 38.1 %collective-permute-start.18 = (f32[1,8,3200]{2,1,0:T(8,128)S(1)}, f32[1,8,3200]{2,1,0:T(8,128)S(1)}, u32[]{:S(2)}, u32[]{:S(2)}) collective-permute-start(f32[1,8,3200]{2,1,0:T(8,128)S(1)} %get-tuple-element.98), channel_id=1, source_target_pairs={{0,8},{1,9},{2,10},{3,11},{4,12},{5,13},{6,14},{7,15},{8,0},{9,1},... | collective-permute-start | bytes 307208 | tf_op jit(solution)/shard_map/ppermute | solution.py:36
  163.3 35.7 %collective-permute-start.20 = (f32[1,8,3200]{2,1,0:T(8,128)S(1)}, f32[1,8,3200]{2,1,0:T(8,128)S(1)}, u32[]{:S(2)}, u32[]{:S(2)}) collective-permute-start(f32[1,8,3200]{2,1,0:T(8,128)S(1)} %get-tuple-element.99), channel_id=1, source_target_pairs={{0,24},{1,25},{2,26},{3,27},{4,28},{5,29},{6,30},{7,31},{8,16},{9,... | collective-permute-start | bytes 307208 | tf_op jit(solution)/shard_map/ppermute | solution.py:36
  175.7 12.4 %collective-permute-start.22 = (f32[4,8,3200]{2,1,0:T(8,128)S(1)}, f32[4,8,3200]{2,1,0:T(8,128)S(1)}, u32[]{:S(2)}, u32[]{:S(2)}) collective-permute-start(f32[4,8,3200]{2,1,0:T(8,128)S(1)} %get-tuple-element.83), channel_id=1, source_target_pairs={{0,2},{1,3},{2,0},{3,1},{4,6},{5,7},{6,4},{7,5},{8,10},{9,11},{10,... | collective-permute-start | bytes 1228808 | tf_op jit(solution)/shard_map/ppermute | solution.py:36
  177.4 15.5 %collective-permute-start.24 = (f32[4,8,3200]{2,1,0:T(8,128)S(1)}, f32[4,8,3200]{2,1,0:T(8,128)S(1)}, u32[]{:S(2)}, u32[]{:S(2)}) collective-permute-start(f32[4,8,3200]{2,1,0:T(8,128)S(1)} %get-tuple-element.84), channel_id=1, source_target_pairs={{0,6},{1,7},{2,4},{3,5},{4,2},{5,3},{6,0},{7,1},{8,14},{9,15},{10,... | collective-permute-start | bytes 1228808 | tf_op jit(solution)/shard_map/ppermute | solution.py:36
  179.4 15.9 %collective-permute-start.23 = (f32[4,8,3200]{2,1,0:T(8,128)S(1)}, f32[4,8,3200]{2,1,0:T(8,128)S(1)}, u32[]{:S(2)}, u32[]{:S(2)}) collective-permute-start(f32[4,8,3200]{2,1,0:T(8,128)S(1)} %get-tuple-element.85), channel_id=1, source_target_pairs={{0,4},{1,5},{2,6},{3,7},{4,0},{5,1},{6,2},{7,3},{8,12},{9,13},{10,... | collective-permute-start | bytes 1228808 | tf_op jit(solution)/shard_map/ppermute | solution.py:36
  188.1 11.0 %collective-permute-start.19 = (f32[1,8,3200]{2,1,0:T(8,128)S(1)}, f32[1,8,3200]{2,1,0:T(8,128)S(1)}, u32[]{:S(2)}, u32[]{:S(2)}) collective-permute-start(f32[1,8,3200]{2,1,0:T(8,128)S(1)} %get-tuple-element.100), channel_id=1, source_target_pairs={{0,16},{1,17},{2,18},{3,19},{4,20},{5,21},{6,22},{7,23},{8,24},{9,... | collective-permute-start | bytes 307208 | tf_op jit(solution)/shard_map/ppermute | solution.py:36
  198.5 9.0 %collective-permute-start.26 = (f32[1,8,3200]{2,1,0:T(8,128)S(1)}, f32[1,8,3200]{2,1,0:T(8,128)S(1)}, u32[]{:S(2)}, u32[]{:S(2)}) collective-permute-start(f32[1,8,3200]{2,1,0:T(8,128)S(1)} %get-tuple-element.97), channel_id=1, source_target_pairs={{0,16},{1,17},{2,18},{3,19},{4,20},{5,21},{6,22},{7,23},{8,24},{9,... | collective-permute-start | bytes 307208 | tf_op jit(solution)/shard_map/ppermute | solution.py:36
  215.6 9.5 %collective-permute-start.40 = (f32[4,16,896]{2,1,0:T(8,128)S(1)}, f32[4,16,896]{2,1,0:T(8,128)S(1)}, u32[]{:S(2)}, u32[]{:S(2)}) collective-permute-start(f32[4,16,896]{2,1,0:T(8,128)S(1)} %pad_maximum_fusion.1), channel_id=1, source_target_pairs={{0,6},{1,7},{2,4},{3,5},{4,2},{5,3},{6,0},{7,1},{8,14},{9,15},{10,... | collective-permute-start | bytes 688136 | tf_op jit(solution)/shard_map/ppermute | solution.py:36
  (64 other events, 301.1 us)

commit v3 on v2

--- a/solution.py
+++ b/solution.py
@@ -35,13 +35,24 @@
     def send(self, x, mask):
         return lax.ppermute(x, AXES, [(i, i ^ mask) for i in range(self.n)])
 
-    def reduce_scatter(self, pieces):
-        for step, (radix, stride) in enumerate(self.stages):
-            if step:
-                x = x.reshape((radix, x.shape[0] // radix) + x.shape[1:])
-                pieces = [x[j] for j in range(radix)]
-            got = [self.send(pieces[j], j * stride) for j in range(1, radix)]
-            x = functools.reduce(jnp.add, got, pieces[0])
+    def spread_out(self, x, step):
+        if step == 0:
+            return x
+        radix = self.stages[step][0]
+        x = x.reshape((radix, x.shape[0] // radix) + x.shape[1:])
+        return [x[j] for j in range(radix)]
+
+    def scatter_send(self, pieces, step):
+        stride = self.stages[step][1]
+        return [self.send(pieces[j], j * stride) for j in range(1, len(pieces))]
+
+    def add_up(self, pieces, got):
+        return functools.reduce(jnp.add, got, pieces[0])
+
+    def scatter_rest(self, x, step):
+        for at in range(step, len(self.stages)):
+            pieces = self.spread_out(x, at)
+            x = self.add_up(pieces, self.scatter_send(pieces, at))
         x = x[0]
         for radix, stride in self.extra:
             while radix > 1:
@@ -49,16 +60,19 @@
                 stride, radix = stride * 2, radix // 2
         return x
 
-    def all_gather(self, x):
-        x = x[None]
-        for radix, stride in self.stages[::-1]:
-            pieces = [x] + [self.send(x, j * stride) for j in range(1, radix)]
-            if (radix, stride) != self.stages[0]:
-                x = jnp.concatenate(pieces)
-        return pieces
-
-    def share(self, x):
-        return lax.all_to_all(x, AXES, 0, 0, tiled=True)
+    def gather_send(self, x, step):
+        radix, stride = self.stages[step]
+        return [self.send(x, j * stride) for j in range(1, radix)]
+
+    def all_reduce(self, x):
+        for radix, stride in self.stages + self.extra:
+            got = [self.send(x, j * stride) for j in range(1, radix)]
+            x = functools.reduce(jnp.add, got, x)
+        return x
+
+
+def tie(*trees):
+    return lax.optimization_barrier(trees)
 
 
 def dot(a, b):
@@ -144,17 +158,13 @@
     to_blocks(scratch, outs, place[0], own, per)
 
 
-def tables_kernel(place, seeds, order, root, high, low, cols, *refs, levels):
-    means, deltas, roots = refs[:levels], refs[levels : 2 * levels], refs[2 * levels :]
-    rows, width = high.shape
+def tables_kernel(place, seeds, order, root, cols, *roots, levels):
     splits = seeds.shape[2]
-    seed_rows, found = seed_columns(seeds, place[1].astype(F32))
+    seed_rows, _ = seed_columns(seeds, place[1].astype(F32))
     order_rows = order[...][:, :splits].astype(F32)
     order_cols = columns_of(order_rows)
-    row = iota((splits, rows), 1).astype(F32)
     lane = iota((splits, splits), 1).astype(F32)
     cluster = iota((splits, root.shape[0]), 1).astype(F32)
-    a, b = high[...], low[...]
     ra, rb = split2(root[...])
     chain, root_at = [], []
     for l in range(levels):
@@ -172,11 +182,34 @@
         root_at.append(node)
         hot = jnp.where(cluster == node, 1.0, 0.0).astype(BF16)
         roots[l][...] = dot(hot, ra) + dot(hot, rb)
+    cols[...] = pack([order_cols[:, l : l + 1] for l in range(levels)] + root_at + chain)
+
+
+def means_kernel(place, seeds, order, member, high, low, *refs, levels, lead, per, own):
+    outs = refs[:lead]
+    means, deltas, wholes = (refs[lead + i * (levels - 1) :][: levels - 1] for i in range(3))
+    scratch = refs[lead + 3 * (levels - 1)]
+    rows, width = high.shape
+    splits = seeds.shape[2]
+    _, found = seed_columns(seeds, place[1].astype(F32))
+    order_cols = columns_of(order[...][:, :splits].astype(F32))
+    row = iota((splits, rows), 1).astype(F32)
+    a, b = high[...], low[...]
+    for l in range(levels):
         hot0, hot1 = halves_hot(found, row, l)
-        d, m = (hot0 - hot1).astype(BF16), (hot0 + hot1).astype(BF16)
-        means[l][...] = dot(m, a) + dot(m, b)
-        deltas[l][...] = dot(d, a) + dot(d, b)
-    cols[...] = pack([order_cols[:, l : l + 1] for l in range(levels)] + root_at + chain)
+        m = (hot0 + hot1).astype(BF16)
+        mean = dot(m, a) + dot(m, b)
+        chosen = order_cols[:, l : l + 1] == member[l : l + 1, :].astype(F32)
+        c = jnp.where(chosen, 1.0, 0.0).astype(BF16)
+        whole = dot(c, a) + dot(c, b)
+        scratch[:, l * width : (l + 1) * width] = mean
+        scratch[:, (levels + l) * width : (levels + l + 1) * width] = whole
+        if l + 1 < levels:
+            d = (hot0 - hot1).astype(BF16)
+            means[l][...] = mean
+            deltas[l][...] = dot(d, a) + dot(d, b)
+            wholes[l][...] = whole
+    to_blocks(scratch, outs, place[0], own, per)
 
 
 def level_step(l, levels, offset, proj, ahead, cols, member, sq, rows_in, lookups, scale):
@@ -214,13 +247,11 @@
     return cols[:, at : at + 1], cols[:, at + 1 : at + 2], cols[:, at + 2 : at + 3]
 
 
-def emit(columns, small, shared):
+def emit(columns, small, across):
     packed = pack(columns)
     small[...] = packed
-    if shared is not None:
-        across = jnp.transpose(packed)[:8, :]
-        for i in range(shared.shape[0]):
-            shared[i] = across
+    if across is not None:
+        across[...] = jnp.transpose(packed)[:8, :]
 
 
 def delta_of(pieces, block, own, per, lo, hi, scratch):
@@ -273,7 +304,7 @@
     proj[...] = project(*split2(d), high[...], low[...])
 
 
-def level_kernel(*refs, l, levels, n, scale):
+def level_kernel(*refs, l, levels, scale):
     refs = list(refs)
     got, proj = refs.pop(0), refs.pop(0)
     ahead = refs.pop(0) if l + 1 < levels else None
@@ -282,9 +313,7 @@
     small, state_out, counts_out, out = (refs.pop(0) for _ in range(4))
     shared = refs.pop(0) if l + 1 < levels else None
     splits = proj.shape[0]
-    total = got[0]
-    for i in range(1, n):
-        total = total + got[i]
+    total = got[...]
     down = columns_of(total)
     counts_out[...] = jnp.zeros(counts_out.shape, F32) if counts is None else counts[...]
     counts_out[2 * (l - 1) : 2 * l, :] = 1.0 / (total[0:2, :] + 1.0)
@@ -330,13 +359,12 @@
 
 def sums_kernel(place, order, *refs, l, levels, lead, per, own):
     refs = list(refs)
+    more = l + 1 < levels
     high, low, state, small = (refs.pop(0) for _ in range(4))
-    more = l + 1 < levels
     if more:
-        mean, delta, start = (refs.pop(0) for _ in range(3))
-    later = [refs.pop(0) for _ in range(levels - 2)] if l == 0 else []
+        whole, mean, delta, start = (refs.pop(0) for _ in range(4))
     outs = [refs.pop(0) for _ in range(lead)]
-    carry_out = refs.pop(0) if l == 0 else None
+    carry_out = refs.pop(0) if l + 2 < levels else None
     scratch = refs.pop(0)
     tables = refs.pop(0) if more else None
     rows, width = high.shape
@@ -344,68 +372,52 @@
     number = iota((splits, rows), 0).astype(F32)
     index = state[1 + 2 * l : 2 + 2 * l, :]
     first = state[2 + 2 * l : 3 + 2 * l, :]
-    chosen = number == index
     a, b = high[...], low[...]
-    for j, f in enumerate((first, 1.0 - first)):
-        wa, wb = split2(jnp.where(chosen, f, 0.0))
-        scratch[:, j * width : (j + 1) * width] = dot(wa, a) + (dot(wa, b) + dot(wb, a))
-    at = 2
+    wa, wb = split2(jnp.where(number == index, first, 0.0))
+    sums = dot(wa, a) + (dot(wa, b) + dot(wb, a))
+    scratch[:, :width] = sums
     if more:
-        m = mean[...]
-        if l:
-            mid = 0.5 * (start[...] * small[:, 6:7] + m)
-            if l == 1:
-                scratch[:, at * width : (at + 1) * width] = mid
-                at += 1
-        else:
-            mid = 0.5 * (start[...] * jnp.where(place[2] == 0, 1.0, 0.0) + m)
-            scratch[:, at * width : (at + 1) * width] = m
-            at += 1
+        factor = small[:, 6:7] if l else jnp.where(place[2] == 0, 1.0, 0.0)
+        mid = 0.5 * (start[...] * factor + mean[...])
         half = 0.5 * delta[...]
-        tables[0] = lanes(scratch, 0, width) + (mid + half)
-        tables[1] = lanes(scratch, 1, width) + (mid - half)
-        first_lane = at * width
+        tables[0] = sums + (mid + half)
+        tables[1] = (whole[...] - sums) + (mid - half)
 
         def move(s, carry):
             node = order[l + 1, s]
             value = tables[lax.rem(node, 2), pl.ds(lax.div(node, 2), 1), :]
-            if l:
-                scratch[pl.ds(s, 1), first_lane : first_lane + width] = value
-            else:
-                carry_out[pl.ds(s, 1), :] = value
+            scratch[pl.ds(s, 1), width : 2 * width] = value
             return carry
 
         lax.fori_loop(0, splits, move, 0, unroll=8)
-        if l:
-            at += 1
-    for ref in later:
-        scratch[:, at * width : (at + 1) * width] = ref[...]
-        at += 1
-    scratch[:, at * width :] = small[...]
+        if carry_out is not None:
+            carry_out[...] = scratch[:, width : 2 * width]
+        scratch[:, 2 * width :] = small[...]
+    else:
+        scratch[:, width:] = small[...]
     to_blocks(scratch, outs, place[0], own, per)
 
 
 def finish_kernel(place, *refs, levels):
     sums = refs[:levels]
-    smalls = refs[levels : 2 * levels - 2]
-    root, delta, out = refs[2 * levels - 2 :]
+    smalls = refs[levels : 2 * levels - 1]
+    early, root, delta, out = refs[2 * levels - 1 :]
     own = out.shape[0] // 2
     width = out.shape[1] - LANES
     here = pl.ds(pl.multiple_of(place[0] * own, 8), own)
     spread = []
     for l in range(levels):
-        if l == 0:
-            mid = 0.5 * (lanes(sums[0], 2, width) + root[here, :])
-        elif l == 1:
-            mid = lanes(sums[1], 2, width)
+        if l:
+            start = lanes(sums[l - 1], 1, width) * smalls[l - 1][here, 6:7]
         else:
-            grown = lanes(sums[l - 1], 3 if l == 2 else 2, width)
-            inverse = smalls[l - 2][here, 6:7]
-            mid = 0.5 * (grown * inverse + lanes(sums[0], l + 1, width))
+            start = root[here, :]
+        mid = 0.5 * (start + lanes(early, l, width))
         half = 0.5 * lanes(delta, l, width)
         last = sums[l].shape[1] - LANES
         for j in range(2):
-            s = lanes(sums[l], j, width)
+            s = lanes(sums[l], 0, width)
+            if j:
+                s = lanes(early, levels + l, width) - s
             count = sums[l][:, last + j : last + j + 1]
             energy = sums[l][:, last + 2 + j : last + 3 + j]
             centre = (s + (mid + half if j == 0 else mid - half)) / (count + 1.0)
@@ -464,10 +476,10 @@
     def struct(shape, dtype=F32):
         return jax.ShapeDtypeStruct(shape, dtype)
 
-    def pieces_of(parts):
-        return [struct((per, own, parts * width + LANES))] * lead
-
-    def call(kernel, name, outs, scalars, args, scratch=(), limit=30):
+    def pieces_of(parts, extra=LANES):
+        return [struct((per, own, parts * width + extra))] * lead
+
+    def call(kernel, name, outs, scalars, args, scratch=(), limit=30, us=3):
         run = pl.pallas_call(
             kernel,
             name=name,
@@ -476,6 +488,9 @@
             out_specs=[vmem] * len(outs),
             scratch_shapes=[pltpu.VMEM(s, F32) for s in scratch],
             compiler_params=pltpu.CompilerParams(vmem_limit_bytes=limit * 1024 * 1024),
+            cost_estimate=pl.CostEstimate(
+                flops=us * 200_000_000, bytes_accessed=0, transcendentals=0
+            ),
         )
         return list(run(*scalars, *args))
 
@@ -488,16 +503,39 @@
         [seeds, embeddings],
         [(splits, levels * width + LANES)],
     )
-    cols, *rest = call(
+    sent_on = comm.scatter_send(sent, 0)
+    cols, *roots = call(
         functools.partial(tables_kernel, levels=levels),
         "tables",
-        [struct(narrow)] + [struct(table)] * (3 * levels),
+        [struct(narrow)] + [struct(table)] * levels,
         [place],
-        [seeds, split_order, root_centroids, high, low],
-    )
-    means, deltas, roots = rest[:levels], rest[levels : 2 * levels], rest[2 * levels :]
-    delta_own = comm.reduce_scatter(sent)
-    pieces = comm.all_gather(delta_own)
+        [seeds, split_order, root_centroids],
+    )
+    sent_on, cols, roots = tie(sent_on, cols, roots)
+    x = comm.spread_out(comm.add_up(sent, sent_on), 1)
+    sent_on = comm.scatter_send(x, 1)
+    early = call(
+        functools.partial(means_kernel, **geometry),
+        "means",
+        pieces_of(2 * levels, 0) + [struct(table)] * (3 * (levels - 1)),
+        [place],
+        [seeds, split_order, member_ids, high, low],
+        [(splits, 2 * levels * width)],
+        us=8,
+    )
+    sent_on, early = tie(sent_on, early)
+    early, rest = early[:lead], early[lead:]
+    means, deltas, wholes = (rest[i * (levels - 1) :][: levels - 1] for i in range(3))
+    delta_own = comm.scatter_rest(comm.add_up(x, sent_on), 2)
+    x = delta_own[None]
+    for step in range(len(comm.stages) - 1, 0, -1):
+        got = comm.gather_send(x, step)
+        if step == 1:
+            early_x = comm.add_up(early, comm.scatter_send(early, 0))
+            got, early_x = tie(got, early_x)
+        x = jnp.concatenate([x] + got)
+    pieces = [x] + comm.gather_send(x, 0)
+    early_own = comm.scatter_rest(early_x, 1)
     proj, stat, small, shared, state, weight = call(
         functools.partial(project_kernel, scale=scale, **geometry),
         "project",
@@ -505,7 +543,7 @@
             struct((splits, rows)),
             struct(narrow),
             struct(narrow),
-            struct((n, 8, splits)),
+            struct((8, splits)),
             struct((8, rows)),
             struct((1, rows)),
         ],
@@ -538,45 +576,48 @@
                 struct((1, rows)),
             ]
             small, state, count, weight, *shared = call(
-                functools.partial(level_kernel, l=l, levels=levels, n=n, scale=scale),
+                functools.partial(level_kernel, l=l, levels=levels, scale=scale),
                 f"level{l}",
-                outs + [struct((n, 8, splits))] * more,
+                outs + [struct((8, splits))] * more,
                 [],
                 [got, *projs[l : l + 2], stat, root_stats[l], small, state, cols, member_ids]
                 + counts,
             )
             counts = [count]
             weights_out.append(weight)
-            if l > 1:
-                smalls.append(small)
+            smalls.append(small)
             shared = shared[0] if more else None
         if more:
-            got = comm.share(shared)
+            got = comm.all_reduce(shared)
         args = [high, low, state, small]
         if more:
-            args += [means[l], deltas[l], start]
-        if l == 0:
-            args += means[2:]
-        parts = 2 + (levels - 1 if l == 0 else (l == 1) + more)
+            args += [wholes[l], means[l], deltas[l], start]
+        parts = 1 + more
         out = call(
             functools.partial(sums_kernel, l=l, **geometry),
             f"sums{l}",
-            pieces_of(parts) + [struct(table)] * (l == 0),
+            pieces_of(parts) + [struct(table)] * (l + 2 < levels),
             [place, split_order],
             args,
             [(splits, parts * width + LANES)] + [(2, splits, width)] * more,
         )
-        if l == 0:
+        if l + 2 < levels:
             start = out.pop()
-        sums_own.append(comm.reduce_scatter(out))
+        x = comm.add_up(out, comm.scatter_send(out, 0))
+        if more:
+            got, x = tie(got, x)
+        sums_own.append(comm.scatter_rest(x, 1))
     (final,) = call(
         functools.partial(finish_kernel, levels=levels),
         "finish",
         [struct((2 * own, width + LANES))],
         [place],
-        [*sums_own, *smalls, roots[0], delta_own],
-    )
-    pieces = comm.all_gather(final)
+        [*sums_own, *smalls, early_own, roots[0], delta_own],
+    )
+    x = final[None]
+    for step in range(len(comm.stages) - 1, 0, -1):
+        x = jnp.concatenate([x] + comm.gather_send(x, step))
+    pieces = [x] + comm.gather_send(x, 0)
     centre, spread = call(
         functools.partial(place_kernel, **geometry),
         "place",

time: 230 us -> 210 us (0.913)
  local copies, waits for them, and re-layouts: 27.4 us -> 3.31 us
  starting transfers between devices: 60.8 us -> 80.6 us
  waiting for transfers between devices: 91 us -> 84.6 us
  Pallas kernels: 44.3 us -> 38.6 us
  other arithmetic: 4.66 us -> 1.93 us
    ppermute x42 -> x63, starting transfers between devices: 53.6 us -> 80.6 us  [send(): return lax.ppermute(x, AXES, [(i, i ^ mask) for i in range(self.n)])]
    unnamed x99 -> x21, local copies, waits for them, and re-layouts: 27.1 us -> 2.72 us
    all_to_all x2 -> x0, starting transfers between devices: 7.19 us -> none  [share(): return lax.all_to_all(x, AXES, 0, 0, tiled=True)]
    pallas_call x11 -> x12, Pallas kernels: 44.3 us -> 38.6 us  [call(): return list(run(*scalars, *args))]
    ppermute x42 -> x63, waiting for transfers between devices: 87.8 us -> 84.6 us  [send(): return lax.ppermute(x, AXES, [(i, i ^ mask) for i in range(self.n)])]
    all_to_all x2 -> x0, waiting for transfers between devices: 3.21 us -> none  [share(): return lax.all_to_all(x, AXES, 0, 0, tiled=True)]
    add x8 -> x16, other arithmetic: 3.8 us -> 1.07 us  [the longest x10 1.03 us: add_up(): return functools.reduce(jnp.add, got, pieces[0])]
  transfers between devices with their start and end apart: 44 -> 63, of which waited for: 30 -> 23; matrix products, arithmetic and copies ran while one was open for 2% -> 1% of each run, Pallas kernels for 11% -> 13%
where the time goes in v3:
time: 210 us
  waiting for transfers between devices  84.6 us (40%)
  starting transfers between devices  80.6 us (38%)
  Pallas kernels  38.6 us (18%)
  local copies, waits for them, and re-layouts  3.31 us (2%)
    ppermute x63, waiting for transfers between devices, send(): return lax.ppermute(x, AXES, [(i, i ^ mask) for i in range(self.n)])  84.6 us
    ppermute x63, starting transfers between devices, send(): return lax.ppermute(x, AXES, [(i, i ^ mask) for i in range(self.n)])  80.6 us
    pallas_call x12, Pallas kernels, call(): return list(run(*scalars, *args))  38.6 us
  transfers between devices with their start and end apart: 63, of which 23 were waited for; matrix products, arithmetic and copies ran while one was open for 1% of the time, Pallas kernels for 13%

profile of v3, /device:TPU:0, one launch (start us, length us, event | category | flops | bytes accessed | tf_op | source)
XLA Modules:
  0.0 210.1 jit_solution(15211125921918039428)
XLA Ops:
  3.4 4.2 %pick.1 = (f32[16,8,2432]{2,1,0:T(8,128)S(1)}, f32[16,8,2432]{2,1,0:T(8,128)S(1)}, bf16[1024,768]{1,0:T(8,128)(2,1)S(1)}, bf16[1024,768]{1,0:T(8,128)(2,1)S(1)}, f32[1,1024]{1,0:T(1,128)S(1)}) custom-call(s32[3]{0:T(128)S(1)} %pad_add_fusion.place, s32[3,2,256]{2,1,0:T(2,128)S(1)} %bitcast.20, f32[1024,768]{1,0:T(8,128)S(1)} %copy-done), custom_call_target="tpu_custom_call" | custom-call | flops 600000000 | tf_op jit(solution)/shard_map/pick/pallas_call | solution.py:495
  10.9 2.9 %collective-permute-start.1 = (f32[4,8,2432]{2,1,0:T(8,128)S(1)}, f32[4,8,2432]{2,1,0:T(8,128)S(1)}, u32[]{:S(2)}, u32[]{:S(2)}) collective-permute-start(f32[4,8,2432]{2,1,0:T(8,128)S(1)} %get-tuple-element.142), channel_id=1, source_target_pairs={{0,2},{1,3},{2,0},{3,1},{4,6},{5,7},{6,4},{7,5},{8,10},{9,11},{10,... | collective-permute-start | bytes 933896 | tf_op jit(solution)/shard_map/ppermute | solution.py:36
  15.4 8.0 %means.1 = (f32[16,8,4608]{2,1,0:T(8,128)S(1)}, f32[16,8,4608]{2,1,0:T(8,128)S(1)}, f32[256,768]{1,0:T(8,128)S(1)}, f32[256,768]{1,0:T(8,128)S(1)}, f32[256,768]...) custom-call(s32[3]{0:T(128)S(1)} %pad_add_fusion.place, ...), custom_call_target="tpu_custom_call" | custom-call | flops 1600000000 | tf_op jit(solution)/shard_map/means/pallas_call | solution.py:495
  23.4 6.2 %collective-permute-done.2 = f32[4,8,2432]{2,1,0:T(8,128)S(1)} collective-permute-done((f32[4,8,2432]{2,1,0:T(8,128)S(1)}, f32[4,8,2432]{2,1,0:T(8,128)S(1)}, u32[]{:S(2)}, u32[]{:S(2)}) %collective-permute-start.2) | collective-permute-done | bytes 311328 | tf_op jit(solution)/shard_map/ppermute | solution.py:36
  31.4 2.6 %collective-permute-start.5 = (f32[1,8,2432]{2,1,0:T(8,128)S(1)}, f32[1,8,2432]{2,1,0:T(8,128)S(1)}, u32[]{:S(2)}, u32[]{:S(2)}) collective-permute-start(f32[1,8,2432]{2,1,0:T(8,128)S(1)} %get-tuple-element.157), channel_id=1, source_target_pairs={{0,16},{1,17},{2,18},{3,19},{4,20},{5,21},{6,22},{7,23},{8,24},{9,... | collective-permute-start | bytes 233480 | tf_op jit(solution)/shard_map/ppermute | solution.py:36
  34.6 6.0 %collective-permute-done.5 = f32[1,8,2432]{2,1,0:T(8,128)S(1)} collective-permute-done((f32[1,8,2432]{2,1,0:T(8,128)S(1)}, f32[1,8,2432]{2,1,0:T(8,128)S(1)}, u32[]{:S(2)}, u32[]{:S(2)}) %collective-permute-start.5) | collective-permute-done | bytes 77856 | tf_op jit(solution)/shard_map/ppermute | solution.py:36
  45.1 6.0 %collective-permute-done.8 = f32[1,8,2432]{2,1,0:T(8,128)S(1)} collective-permute-done((f32[1,8,2432]{2,1,0:T(8,128)S(1)}, f32[1,8,2432]{2,1,0:T(8,128)S(1)}, u32[]{:S(2)}, u32[]{:S(2)}) %collective-permute-start.8) | collective-permute-done | bytes 77856 | tf_op jit(solution)/shard_map/ppermute | solution.py:36
  54.9 6.3 %collective-permute-done.10 = f32[4,8,2432]{2,1,0:T(8,128)S(1)} collective-permute-done((f32[4,8,2432]{2,1,0:T(8,128)S(1)}, f32[4,8,2432]{2,1,0:T(8,128)S(1)}, u32[]{:S(2)}, u32[]{:S(2)}) %collective-permute-start.10) | collective-permute-done | bytes 311328 | tf_op jit(solution)/shard_map/ppermute | solution.py:36
  61.2 3.7 %collective-permute-done.11 = f32[4,8,2432]{2,1,0:T(8,128)S(1)} collective-permute-done((f32[4,8,2432]{2,1,0:T(8,128)S(1)}, f32[4,8,2432]{2,1,0:T(8,128)S(1)}, u32[]{:S(2)}, u32[]{:S(2)}) %collective-permute-start.11) | collective-permute-done | bytes 311328 | tf_op jit(solution)/shard_map/ppermute | solution.py:36
  70.4 12.5 %collective-permute-done.50 = f32[4,8,4608]{2,1,0:T(8,128)S(1)} collective-permute-done((f32[4,8,4608]{2,1,0:T(8,128)S(1)}, f32[4,8,4608]{2,1,0:T(8,128)S(1)}, u32[]{:S(2)}, u32[]{:S(2)}) %collective-permute-start.50) | collective-permute-done | bytes 589856 | tf_op jit(solution)/shard_map/ppermute | solution.py:36
  82.9 8.0 %collective-permute-done.51 = f32[4,8,4608]{2,1,0:T(8,128)S(1)} collective-permute-done((f32[4,8,4608]{2,1,0:T(8,128)S(1)}, f32[4,8,4608]{2,1,0:T(8,128)S(1)}, u32[]{:S(2)}, u32[]{:S(2)}) %collective-permute-start.51) | collective-permute-done | bytes 589856 | tf_op jit(solution)/shard_map/ppermute | solution.py:36
  91.1 4.2 %project.1 = (f32[256,1024]{1,0:T(8,128)S(1)}, f32[256,128]{1,0:T(8,128)S(1)}, f32[256,128]{1,0:T(8,128)S(1)}, f32[8,256]{1,0:T(8,128)S(1)}, f32[8,1024]{1,0:T(8,128)S(1)}, /*index=5*/f32[1,1024]{1,0:T(1,128)S(1)}) custom-call(s32[3]{0:T(128)S(1)} %pad_add_fusion.place, f32[16,8,2432]{2,1,0:T(8,128)S(1)} %constant_dynamic-update-slice_fusion.refs_0_, ...), custom_call_target="tpu_custom_call" | custom-call | flops 600000000 | tf_op jit(solution)/shard_map/project/pallas_call | solution.py:495
  95.4 4.5 %sums0.1 = (f32[16,8,1664]{2,1,0:T(8,128)S(1)}, f32[16,8,1664]{2,1,0:T(8,128)S(1)}, f32[256,768]{1,0:T(8,128)S(1)}) custom-call(s32[3]{0:T(128)S(1)} %pad_add_fusion.place, s32[3,512]{1,0:T(4,128)S(1)} %copy-done.1, bf16[1024,768]{1,0:T(8,128)(2,1)S(1)} %get-tuple-element.76.high.refs_2_.refs_0_, ...), custom_call_target="tpu_custom_call" | custom-call | flops 600000000 | tf_op jit(solution)/shard_map/sums0/pallas_call | solution.py:495
  104.0 4.9 %collective-permute-start.53 = (f32[1,8,4608]{2,1,0:T(8,128)S(1)}, f32[1,8,4608]{2,1,0:T(8,128)S(1)}, u32[]{:S(2)}, u32[]{:S(2)}) collective-permute-start(f32[1,8,4608]{2,1,0:T(8,128)S(1)} %get-tuple-element.149), channel_id=1, source_target_pairs={{0,8},{1,9},{2,10},{3,11},{4,12},{5,13},{6,14},{7,15},{8,0},{9,1},... | collective-permute-start | bytes 442376 | tf_op jit(solution)/shard_map/ppermute | solution.py:36
  108.9 2.9 %collective-permute-start.19 = (f32[8,256]{1,0:T(8,128)S(1)}, f32[8,256]{1,0:T(8,128)S(1)}, u32[]{:S(2)}, u32[]{:S(2)}) collective-permute-start(f32[8,256]{1,0:T(8,128)S(1)} %add_add_fusion.6), channel_id=1, source_target_pairs={{0,8},{1,9},{2,10},{3,11},{4,12},{5,13},{6,14},{7,15},{8,0},{9,1},... | collective-permute-start | bytes 24584 | tf_op jit(solution)/shard_map/ppermute | solution.py:36
  122.4 5.2 %collective-permute-done.54 = f32[1,8,4608]{2,1,0:T(8,128)S(1)} collective-permute-done((f32[1,8,4608]{2,1,0:T(8,128)S(1)}, f32[1,8,4608]{2,1,0:T(8,128)S(1)}, u32[]{:S(2)}, u32[]{:S(2)}) %collective-permute-start.54) | collective-permute-done | bytes 147488 | tf_op jit(solution)/shard_map/ppermute | solution.py:36
  131.2 4.7 %sums1.1 = (f32[16,8,1664]{2,1,0:T(8,128)S(1)}, f32[16,8,1664]{2,1,0:T(8,128)S(1)}) custom-call(s32[3]{0:T(128)S(1)} %pad_add_fusion.place, s32[3,512]{1,0:T(4,128)S(1)} %copy-done.1, bf16[1024,768]{1,0:T(8,128)(2,1)S(1)} %get-tuple-element.76.high.refs_2_.refs_0_, bf16[1024,768]{1,0:T(8,128)(2,1)S(1)} %get-tuple-element.77.low.refs_3_.refs_1_, ...), custom_call_target="tpu_custom_call" | custom-call | flops 600000000 | tf_op jit(solution)/shard_map/sums1/pallas_call | solution.py:495
  136.1 3.5 %collective-permute-start.33 = (f32[8,256]{1,0:T(8,128)S(1)}, f32[8,256]{1,0:T(8,128)S(1)}, u32[]{:S(2)}, u32[]{:S(2)}) collective-permute-start(f32[8,256]{1,0:T(8,128)S(1)} %add_add_fusion.4), channel_id=1, source_target_pairs={{0,8},{1,9},{2,10},{3,11},{4,12},{5,13},{6,14},{7,15},{8,0},{9,1},... | collective-permute-start | bytes 24584 | tf_op jit(solution)/shard_map/ppermute | solution.py:36
  145.6 4.6 %collective-permute-done.23 = f32[4,8,1664]{2,1,0:T(8,128)S(1)} collective-permute-done((f32[4,8,1664]{2,1,0:T(8,128)S(1)}, f32[4,8,1664]{2,1,0:T(8,128)S(1)}, u32[]{:S(2)}, u32[]{:S(2)}) %collective-permute-start.23) | collective-permute-done | bytes 213024 | tf_op jit(solution)/shard_map/ppermute | solution.py:36
  151.1 3.5 %collective-permute-done.25 = f32[4,8,1664]{2,1,0:T(8,128)S(1)} collective-permute-done((f32[4,8,1664]{2,1,0:T(8,128)S(1)}, f32[4,8,1664]{2,1,0:T(8,128)S(1)}, u32[]{:S(2)}, u32[]{:S(2)}) %collective-permute-start.25) | collective-permute-done | bytes 213024 | tf_op jit(solution)/shard_map/ppermute | solution.py:36
  167.0 2.7 %collective-permute-done.38 = f32[4,8,1664]{2,1,0:T(8,128)S(1)} collective-permute-done((f32[4,8,1664]{2,1,0:T(8,128)S(1)}, f32[4,8,1664]{2,1,0:T(8,128)S(1)}, u32[]{:S(2)}, u32[]{:S(2)}) %collective-permute-start.38) | collective-permute-done | bytes 213024 | tf_op jit(solution)/shard_map/ppermute | solution.py:36
  182.9 3.5 %collective-permute-done.49 = f32[1,8,896]{2,1,0:T(8,128)S(1)} collective-permute-done((f32[1,8,896]{2,1,0:T(8,128)S(1)}, f32[1,8,896]{2,1,0:T(8,128)S(1)}, u32[]{:S(2)}, u32[]{:S(2)}) %collective-permute-start.49) | collective-permute-done | bytes 28704 | tf_op jit(solution)/shard_map/ppermute | solution.py:36
  192.4 3.1 %collective-permute-done.58 = f32[1,16,896]{2,1,0:T(8,128)S(1)} collective-permute-done((f32[1,16,896]{2,1,0:T(8,128)S(1)}, f32[1,16,896]{2,1,0:T(8,128)S(1)}, u32[]{:S(2)}, u32[]{:S(2)}) %collective-permute-start.58) | collective-permute-done | bytes 57376 | tf_op jit(solution)/shard_map/ppermute | solution.py:36
  201.7 4.1 %collective-permute-done.60 = f32[4,16,896]{2,1,0:T(8,128)S(1)} collective-permute-done((f32[4,16,896]{2,1,0:T(8,128)S(1)}, f32[4,16,896]{2,1,0:T(8,128)S(1)}, u32[]{:S(2)}, u32[]{:S(2)}) %collective-permute-start.60) | collective-permute-done | bytes 229408 | tf_op jit(solution)/shard_map/ppermute | solution.py:36
  (172 shorter events, 91.1 us)
Async XLA Ops:
  10.9 12.5 %collective-permute-start.1 = (f32[4,8,2432]{2,1,0:T(8,128)S(1)}, f32[4,8,2432]{2,1,0:T(8,128)S(1)}, u32[]{:S(2)}, u32[]{:S(2)}) collective-permute-start(f32[4,8,2432]{2,1,0:T(8,128)S(1)} %get-tuple-element.142), channel_id=1, source_target_pairs={{0,2},{1,3},{2,0},{3,1},{4,6},{5,7},{6,4},{7,5},{8,10},{9,11},{10,... | collective-permute-start | bytes 933896 | tf_op jit(solution)/shard_map/ppermute | solution.py:36
  13.8 15.8 %collective-permute-start.2 = (f32[4,8,2432]{2,1,0:T(8,128)S(1)}, f32[4,8,2432]{2,1,0:T(8,128)S(1)}, u32[]{:S(2)}, u32[]{:S(2)}) collective-permute-start(f32[4,8,2432]{2,1,0:T(8,128)S(1)} %get-tuple-element.141), channel_id=1, source_target_pairs={{0,4},{1,5},{2,6},{3,7},{4,0},{5,1},{6,2},{7,3},{8,12},{9,13},{10,... | collective-permute-start | bytes 933896 | tf_op jit(solution)/shard_map/ppermute | solution.py:36
  15.4 14.3 %collective-permute-start.3 = (f32[4,8,2432]{2,1,0:T(8,128)S(1)}, f32[4,8,2432]{2,1,0:T(8,128)S(1)}, u32[]{:S(2)}, u32[]{:S(2)}) collective-permute-start(f32[4,8,2432]{2,1,0:T(8,128)S(1)} %get-tuple-element.140), channel_id=1, source_target_pairs={{0,6},{1,7},{2,4},{3,5},{4,2},{5,3},{6,0},{7,1},{8,14},{9,15},{10,... | collective-permute-start | bytes 933896 | tf_op jit(solution)/shard_map/ppermute | solution.py:36
  29.6 25.1 %collective-permute-start.13 = (f32[16,8,4608]{2,1,0:T(8,128)S(1)}, f32[16,8,4608]{2,1,0:T(8,128)S(1)}, u32[]{:S(2)}, u32[]{:S(2)}) collective-permute-start(f32[16,8,4608]{2,1,0:T(8,128)S(1)} %get-tuple-element.90), channel_id=1, source_target_pairs={{0,1},{1,0},{2,3},{3,2},{4,5},{5,4},{6,7},{7,6},{8,9},{9,8},{10,11... | collective-permute-start | bytes 7077896 | tf_op jit(solution)/shard_map/ppermute | solution.py:36
  31.4 9.2 %collective-permute-start.5 = (f32[1,8,2432]{2,1,0:T(8,128)S(1)}, f32[1,8,2432]{2,1,0:T(8,128)S(1)}, u32[]{:S(2)}, u32[]{:S(2)}) collective-permute-start(f32[1,8,2432]{2,1,0:T(8,128)S(1)} %get-tuple-element.157), channel_id=1, source_target_pairs={{0,16},{1,17},{2,18},{3,19},{4,20},{5,21},{6,22},{7,23},{8,24},{9,... | collective-permute-start | bytes 233480 | tf_op jit(solution)/shard_map/ppermute | solution.py:36
  42.4 8.6 %collective-permute-start.8 = (f32[1,8,2432]{2,1,0:T(8,128)S(1)}, f32[1,8,2432]{2,1,0:T(8,128)S(1)}, u32[]{:S(2)}, u32[]{:S(2)}) collective-permute-start(f32[1,8,2432]{2,1,0:T(8,128)S(1)} %get-tuple-element.136), channel_id=1, source_target_pairs={{0,16},{1,17},{2,18},{3,19},{4,20},{5,21},{6,22},{7,23},{8,24},{9,... | collective-permute-start | bytes 233480 | tf_op jit(solution)/shard_map/ppermute | solution.py:36
  51.1 10.1 %collective-permute-start.10 = (f32[4,8,2432]{2,1,0:T(8,128)S(1)}, f32[4,8,2432]{2,1,0:T(8,128)S(1)}, u32[]{:S(2)}, u32[]{:S(2)}) collective-permute-start(f32[4,8,2432]{2,1,0:T(8,128)S(1)} %pad_maximum_fusion), channel_id=1, source_target_pairs={{0,2},{1,3},{2,0},{3,1},{4,6},{5,7},{6,4},{7,5},{8,10},{9,11},{10,... | collective-permute-start | bytes 933896 | tf_op jit(solution)/shard_map/ppermute | solution.py:36
  52.4 12.5 %collective-permute-start.11 = (f32[4,8,2432]{2,1,0:T(8,128)S(1)}, f32[4,8,2432]{2,1,0:T(8,128)S(1)}, u32[]{:S(2)}, u32[]{:S(2)}) collective-permute-start(f32[4,8,2432]{2,1,0:T(8,128)S(1)} %pad_maximum_fusion), channel_id=1, source_target_pairs={{0,4},{1,5},{2,6},{3,7},{4,0},{5,1},{6,2},{7,3},{8,12},{9,13},{10,... | collective-permute-start | bytes 933896 | tf_op jit(solution)/shard_map/ppermute | solution.py:36
  53.2 13.1 %collective-permute-start.12 = (f32[4,8,2432]{2,1,0:T(8,128)S(1)}, f32[4,8,2432]{2,1,0:T(8,128)S(1)}, u32[]{:S(2)}, u32[]{:S(2)}) collective-permute-start(f32[4,8,2432]{2,1,0:T(8,128)S(1)} %pad_maximum_fusion), channel_id=1, source_target_pairs={{0,6},{1,7},{2,4},{3,5},{4,2},{5,3},{6,0},{7,1},{8,14},{9,15},{10,... | collective-permute-start | bytes 933896 | tf_op jit(solution)/shard_map/ppermute | solution.py:36
  66.7 16.3 %collective-permute-start.50 = (f32[4,8,4608]{2,1,0:T(8,128)S(1)}, f32[4,8,4608]{2,1,0:T(8,128)S(1)}, u32[]{:S(2)}, u32[]{:S(2)}) collective-permute-start(f32[4,8,4608]{2,1,0:T(8,128)S(1)} %get-tuple-element.137), channel_id=1, source_target_pairs={{0,2},{1,3},{2,0},{3,1},{4,6},{5,7},{6,4},{7,5},{8,10},{9,11},{10,... | collective-permute-start | bytes 1769480 | tf_op jit(solution)/shard_map/ppermute | solution.py:36
  66.7 24.2 %collective-permute-start.51 = (f32[4,8,4608]{2,1,0:T(8,128)S(1)}, f32[4,8,4608]{2,1,0:T(8,128)S(1)}, u32[]{:S(2)}, u32[]{:S(2)}) collective-permute-start(f32[4,8,4608]{2,1,0:T(8,128)S(1)} %get-tuple-element.139), channel_id=1, source_target_pairs={{0,4},{1,5},{2,6},{3,7},{4,0},{5,1},{6,2},{7,3},{8,12},{9,13},{10,... | collective-permute-start | bytes 1769480 | tf_op jit(solution)/shard_map/ppermute | solution.py:36
  68.6 22.4 %collective-permute-start.52 = (f32[4,8,4608]{2,1,0:T(8,128)S(1)}, f32[4,8,4608]{2,1,0:T(8,128)S(1)}, u32[]{:S(2)}, u32[]{:S(2)}) collective-permute-start(f32[4,8,4608]{2,1,0:T(8,128)S(1)} %get-tuple-element.138), channel_id=1, source_target_pairs={{0,6},{1,7},{2,4},{3,5},{4,2},{5,3},{6,0},{7,1},{8,14},{9,15},{10,... | collective-permute-start | bytes 1769480 | tf_op jit(solution)/shard_map/ppermute | solution.py:36
  70.3 20.8 %collective-permute-start.14 = (f32[16,8,2432]{2,1,0:T(8,128)S(1)}, f32[16,8,2432]{2,1,0:T(8,128)S(1)}, u32[]{:S(2)}, u32[]{:S(2)}) collective-permute-start(f32[16,8,2432]{2,1,0:T(8,128)S(1)} %constant_dynamic-update-slice_fusion.refs_0_), channel_id=1, source_target_pairs={{0,1},{1,0},{2,3},{3,2},{4,5},{5,4},{6,7},{7,6},{8,9},{9,8},{10,11... | collective-permute-start | bytes 3735560 | tf_op jit(solution)/shard_map/ppermute | solution.py:36
  99.9 19.9 %collective-permute-start.22 = (f32[16,8,1664]{2,1,0:T(8,128)S(1)}, f32[16,8,1664]{2,1,0:T(8,128)S(1)}, u32[]{:S(2)}, u32[]{:S(2)}) collective-permute-start(f32[16,8,1664]{2,1,0:T(8,128)S(1)} %get-tuple-element.105), channel_id=1, source_target_pairs={{0,1},{1,0},{2,3},{3,2},{4,5},{5,4},{6,7},{7,6},{8,9},{9,8},{10,11... | collective-permute-start | bytes 2555912 | tf_op jit(solution)/shard_map/ppermute | solution.py:36
  100.5 8.4 %collective-permute-start.16 = (f32[8,256]{1,0:T(8,128)S(1)}, f32[8,256]{1,0:T(8,128)S(1)}, u32[]{:S(2)}, u32[]{:S(2)}) collective-permute-start(f32[8,256]{1,0:T(8,128)S(1)} %add.183), channel_id=1, source_target_pairs={{0,2},{1,3},{2,0},{3,1},{4,6},{5,7},{6,4},{7,5},{8,10},{9,11},{10,... | collective-permute-start | bytes 24584 | tf_op jit(solution)/shard_map/ppermute | solution.py:36
  104.0 18.4 %collective-permute-start.53 = (f32[1,8,4608]{2,1,0:T(8,128)S(1)}, f32[1,8,4608]{2,1,0:T(8,128)S(1)}, u32[]{:S(2)}, u32[]{:S(2)}) collective-permute-start(f32[1,8,4608]{2,1,0:T(8,128)S(1)} %get-tuple-element.149), channel_id=1, source_target_pairs={{0,8},{1,9},{2,10},{3,11},{4,12},{5,13},{6,14},{7,15},{8,0},{9,1},... | collective-permute-start | bytes 442376 | tf_op jit(solution)/shard_map/ppermute | solution.py:36
  116.4 11.3 %collective-permute-start.54 = (f32[1,8,4608]{2,1,0:T(8,128)S(1)}, f32[1,8,4608]{2,1,0:T(8,128)S(1)}, u32[]{:S(2)}, u32[]{:S(2)}) collective-permute-start(f32[1,8,4608]{2,1,0:T(8,128)S(1)} %get-tuple-element.151), channel_id=1, source_target_pairs={{0,16},{1,17},{2,18},{3,19},{4,20},{5,21},{6,22},{7,23},{8,24},{9,... | collective-permute-start | bytes 442376 | tf_op jit(solution)/shard_map/ppermute | solution.py:36
  117.4 10.2 %collective-permute-start.55 = (f32[1,8,4608]{2,1,0:T(8,128)S(1)}, f32[1,8,4608]{2,1,0:T(8,128)S(1)}, u32[]{:S(2)}, u32[]{:S(2)}) collective-permute-start(f32[1,8,4608]{2,1,0:T(8,128)S(1)} %get-tuple-element.150), channel_id=1, source_target_pairs={{0,24},{1,25},{2,26},{3,27},{4,28},{5,29},{6,30},{7,31},{8,16},{9,... | collective-permute-start | bytes 442376 | tf_op jit(solution)/shard_map/ppermute | solution.py:36
  127.7 8.4 %collective-permute-start.30 = (f32[8,256]{1,0:T(8,128)S(1)}, f32[8,256]{1,0:T(8,128)S(1)}, u32[]{:S(2)}, u32[]{:S(2)}) collective-permute-start(f32[8,256]{1,0:T(8,128)S(1)} %add.197), channel_id=1, source_target_pairs={{0,2},{1,3},{2,0},{3,1},{4,6},{5,7},{6,4},{7,5},{8,10},{9,11},{10,... | collective-permute-start | bytes 24584 | tf_op jit(solution)/shard_map/ppermute | solution.py:36
  136.0 23.2 %collective-permute-start.36 = (f32[16,8,1664]{2,1,0:T(8,128)S(1)}, f32[16,8,1664]{2,1,0:T(8,128)S(1)}, u32[]{:S(2)}, u32[]{:S(2)}) collective-permute-start(f32[16,8,1664]{2,1,0:T(8,128)S(1)} %get-tuple-element.120), channel_id=1, source_target_pairs={{0,1},{1,0},{2,3},{3,2},{4,5},{5,4},{6,7},{7,6},{8,9},{9,8},{10,11... | collective-permute-start | bytes 2555912 | tf_op jit(solution)/shard_map/ppermute | solution.py:36
  144.1 10.5 %collective-permute-start.25 = (f32[4,8,1664]{2,1,0:T(8,128)S(1)}, f32[4,8,1664]{2,1,0:T(8,128)S(1)}, u32[]{:S(2)}, u32[]{:S(2)}) collective-permute-start(f32[4,8,1664]{2,1,0:T(8,128)S(1)} %get-tuple-element.147), channel_id=1, source_target_pairs={{0,6},{1,7},{2,4},{3,5},{4,2},{5,3},{6,0},{7,1},{8,14},{9,15},{10,... | collective-permute-start | bytes 638984 | tf_op jit(solution)/shard_map/ppermute | solution.py:36
  160.3 9.4 %collective-permute-start.38 = (f32[4,8,1664]{2,1,0:T(8,128)S(1)}, f32[4,8,1664]{2,1,0:T(8,128)S(1)}, u32[]{:S(2)}, u32[]{:S(2)}) collective-permute-start(f32[4,8,1664]{2,1,0:T(8,128)S(1)} %get-tuple-element.145), channel_id=1, source_target_pairs={{0,4},{1,5},{2,6},{3,7},{4,0},{5,1},{6,2},{7,3},{8,12},{9,13},{10,... | collective-permute-start | bytes 638984 | tf_op jit(solution)/shard_map/ppermute | solution.py:36
  173.6 8.9 %collective-permute-start.41 = (f32[1,8,1664]{2,1,0:T(8,128)S(1)}, f32[1,8,1664]{2,1,0:T(8,128)S(1)}, u32[]{:S(2)}, u32[]{:S(2)}) collective-permute-start(f32[1,8,1664]{2,1,0:T(8,128)S(1)} %get-tuple-element.160), channel_id=1, source_target_pairs={{0,16},{1,17},{2,18},{3,19},{4,20},{5,21},{6,22},{7,23},{8,24},{9,... | collective-permute-start | bytes 159752 | tf_op jit(solution)/shard_map/ppermute | solution.py:36
  197.3 8.5 %collective-permute-start.60 = (f32[4,16,896]{2,1,0:T(8,128)S(1)}, f32[4,16,896]{2,1,0:T(8,128)S(1)}, u32[]{:S(2)}, u32[]{:S(2)}) collective-permute-start(f32[4,16,896]{2,1,0:T(8,128)S(1)} %pad_maximum_fusion.1), channel_id=1, source_target_pairs={{0,4},{1,5},{2,6},{3,7},{4,0},{5,1},{6,2},{7,3},{8,12},{9,13},{10,... | collective-permute-start | bytes 688136 | tf_op jit(solution)/shard_map/ppermute | solution.py:36
  (44 other events, 254.1 us)
